TPU v7x, 512 devices: a 4x2x32 block of a 4x8x32 slice. The times are simulated.
512 devices in a mesh: grp: 2 (over y), seq: 32 (over z), head: 4 (over x), rep: 2 (over core).
Axes of the slice: x: 4, y: 2, z: 32, core: 2. Of those that a mesh axis runs over, the one named last changes fastest.
The devices are a block of a 4x8x32 slice.
Arguments:
- x_proj: bfloat16 [4, 32, 32, 4, 8192], P(('grp', 'rep'), None, 'seq', None, 'head'), parts along dimension 0, may hold values from -6 to 6
- gate_proj: bfloat16 [4, 32, 32, 4, 8192], P(('grp', 'rep'), None, 'seq', None, 'head'), parts along dimension 0, may hold values from -6 to 6
- bc_proj: bfloat16 [4, 32, 32, 4, 256], P(('grp', 'rep'), None, 'seq'), parts along dimension 0, may hold values from -6 to 6
- dt_proj: bfloat16 [4, 32, 32, 4, 128], P(('grp', 'rep'), None, 'seq', None, 'head'), parts along dimension 0, may hold values from -5.5 to 7.5
- a_rate: float32 [128], P('head'), may hold values from 2.4414063e-05 to 0.05
- dt_bias: float32 [128], P('head'), may hold values from -1 to 1
- d_skip: float32 [128], P('head'), may hold values from 0.5 to 1.5
- conv_x_weight: float32 [4, 8192], P(None, 'head'), may hold values from -3 to 3
- conv_bc_weight: float32 [4, 256], replicated, may hold values from -3 to 3
- norm_gain: float32 [8192], P('head'), may hold values from 0.1 to 1.9
- out_weight: bfloat16 [8192, 2048], P(('seq', 'rep'), 'head'), may hold values from -0.0625 to 0.0625
- request_first_position: int32 [4], P(('grp', 'rep')), parts along dimension 0, may hold values from 0 to 2047
- owner: int32 [4, 32], P(('grp', 'rep')), parts along dimension 0, may hold values from 0 to 31, each once within a row
Outputs:
- mixed: bfloat16 [4, 4096, 2048], P(('grp', 'rep'), 'seq', 'head'), parts along dimension 0
- ssm_state: float32 [4, 32, 128, 256], P(('grp', 'rep'), 'seq', 'head'), parts along dimension 0
- conv_x_state: bfloat16 [4, 32, 3, 256], P(('grp', 'rep'), 'seq', None, 'head'), parts along dimension 0
- conv_bc_state: bfloat16 [4, 32, 3, 8], P(('grp', 'rep'), 'seq'), parts along dimension 0
There are 2 independent parts, one for each index of `grp`. A program takes and returns all parts, laid end to end along the dimension named above; an argument that names none is the same for every part. Nothing has to cross between parts.
Inputs may be any that keep to these rules, and one draw needn't show every extreme that they name: Each row of owner names every index of seq once.
All inputs are finite; a program needn't handle non-finite values.
Results may differ from a plain program's by a relative error of at most 0.007.
Values may be sent and summed in bfloat16 or wider, within the bound.
A program may use at most 128 MiB of HBM per device.

v0:
```python
import jax
import jax.numpy as jnp
from jax import lax
from jax.sharding import PartitionSpec as P

HEAD_DIM = 64
NSTATE = 128
KCONV = 4
SPAN = 128
INNER = 8192


highest = lax.Precision.HIGHEST
stability_constant = 1e-05


def side_by_side(arrays, axis, split_dim, concat_dim, along):
    ends, at = ([], 0)
    for a in arrays[:-1]:
        at += a.shape[along]
        ends.append(at)
    both = jnp.concatenate(arrays, axis=along)
    return tuple(
        jnp.split(
            lax.all_to_all(both, axis, split_axis=split_dim, concat_axis=concat_dim, tiled=True),
            ends,
            axis=along,
        )
    )


def passed_along(value, axis, by):
    devices = lax.axis_size(axis)
    pairs = [(i, i + by) for i in range(devices) if 0 <= i + by < devices]
    return lax.ppermute(value, axis, pairs)


def prefix(value, axis, combine, identity):
    devices, place = (lax.axis_size(axis), lax.axis_index(axis))
    everything = jax.tree.map(lambda part: lax.all_gather(part, axis), value)
    start = jax.tree.map(
        lambda part, zero: jnp.broadcast_to(jnp.asarray(zero, part.dtype), part.shape),
        value,
        identity,
    )

    def lap(k, before):
        reached = k < place
        new = combine(before, jax.tree.map(lambda part: part[k], everything))
        return jax.tree.map(lambda a, b: jnp.where(reached, a, b), new, before)

    return lax.fori_loop(0, devices, lap, start)


def broadcast(block, axis, source):
    block = jnp.where(lax.axis_index(axis) == source, block, jnp.zeros_like(block))
    return lax.psum(block, axis)


def span_terms(x_conv, b_rows, c_rows, step_size, log_decay):
    cum_decay = jnp.cumsum(log_decay, axis=1)
    scores = jnp.einsum("kqn,ktn->kqt", c_rows, b_rows, preferred_element_type=jnp.float32)
    cum_heads = jnp.swapaxes(cum_decay, 1, 2)
    step_heads = jnp.swapaxes(step_size, 1, 2)
    block_len = cum_decay.shape[1]
    causal = jnp.arange(block_len)[:, None] >= jnp.arange(block_len)[None, :]
    decay_gap = cum_heads[:, :, :, None] - cum_heads[:, :, None, :]
    seg_decay = jnp.exp(jnp.where(causal, decay_gap, -jnp.inf))
    weights = (scores[:, None] * seg_decay * step_heads[:, :, None, :]).astype(jnp.bfloat16)
    y_intra = jnp.einsum("khqt,kthp->kqhp", weights, x_conv, preferred_element_type=jnp.float32)
    remaining_length = jnp.exp(cum_decay[:, -1:, :] - cum_decay)
    scaled = ((remaining_length * step_size)[..., None] * x_conv.astype(jnp.float32)).astype(
        jnp.bfloat16
    )
    states = jnp.einsum("kthp,ktn->khpn", scaled, b_rows, preferred_element_type=jnp.float32)
    return (cum_decay, y_intra, states, jnp.exp(cum_decay[:, -1, :]))


def conv_silu(preceding_tokens, current, weight):
    extended = jnp.concatenate([preceding_tokens, current], axis=0)
    length = current.shape[0]
    accum = jnp.zeros(current.shape, jnp.float32)
    for offset in range(weight.shape[0]):
        accum = accum + weight[offset] * extended[offset : offset + length].astype(jnp.float32)
    return jax.nn.silu(accum)


def link(preceding_tokens, later):
    return (
        preceding_tokens[0] * later[0],
        later[0][:, None, None] * preceding_tokens[1] + later[1],
    )


def add_rows(source, piece):
    return jnp.dot(source, piece, preferred_element_type=jnp.float32)


def take_slab(values, slab_index, seq_count):
    grouped = values.reshape(values.shape[0], seq_count, -1)
    return lax.dynamic_index_in_dim(grouped, slab_index, axis=1, keepdims=False)


def local(
    x_proj,
    gate_proj,
    bc_proj,
    dt_proj,
    a_rate,
    dt_bias,
    d_skip,
    conv_x_weight,
    conv_bc_weight,
    norm_gain,
    out_weight,
    request_first_position,
    owner,
):
    x_all, z_all, bc_all, dt_all = side_by_side(
        (x_proj, gate_proj, bc_proj, dt_proj), "seq", 1, 2, 4
    )
    tokens_here = x_all.shape[2] * x_all.shape[3]
    x_local = x_all.reshape(tokens_here, x_all.shape[4])
    z_local = z_all.reshape(tokens_here, z_all.shape[4])
    bc_local = bc_all.reshape(tokens_here, bc_all.shape[4])
    dt_local = dt_all.reshape(tokens_here, dt_all.shape[4])
    heads = dt_local.shape[1]
    seq_index = lax.axis_index("seq")
    seq_count = lax.axis_size("seq")
    positions = seq_index * tokens_here + jnp.arange(tokens_here, dtype=jnp.int32)
    is_live = positions >= request_first_position[0]
    x_live = jnp.where(is_live[:, None], x_local, jnp.zeros_like(x_local))
    bc_live = jnp.where(is_live[:, None], bc_local, jnp.zeros_like(bc_local))
    rim_rows = KCONV - 1
    tail_x = x_live[tokens_here - rim_rows :]
    tail_bc = bc_live[tokens_here - rim_rows :]
    before_x, before_bc = passed_along((tail_x, tail_bc), "seq", 1)
    x_conv = conv_silu(before_x, x_live, conv_x_weight).astype(jnp.bfloat16)
    bc_conv = conv_silu(before_bc, bc_live, conv_bc_weight).astype(jnp.bfloat16)
    step_size = (
        jax.nn.softplus(dt_local.astype(jnp.float32) + dt_bias)
        * is_live.astype(jnp.float32)[:, None]
    )
    log_decay = -a_rate * step_size
    blocks = tokens_here // SPAN
    x_blocks = x_conv.reshape(blocks, SPAN, heads, HEAD_DIM)
    b_blocks = bc_conv[:, :NSTATE].reshape(blocks, SPAN, NSTATE)
    c_blocks = bc_conv[:, NSTATE:].reshape(blocks, SPAN, NSTATE)
    cum_decay, y_intra, states, decays = span_terms(
        x_blocks,
        b_blocks,
        c_blocks,
        step_size.reshape(blocks, SPAN, heads),
        log_decay.reshape(blocks, SPAN, heads),
    )

    def advance(carry, inputs):
        factor, contrib = inputs
        return (factor[:, None, None] * carry + contrib, carry)

    zero_state = jnp.zeros((heads, HEAD_DIM, NSTATE), jnp.float32)
    local_final, local_enter = lax.scan(advance, zero_state, (decays, states))
    dev_decay = jnp.prod(decays, axis=0)
    ones_heads = jnp.ones((heads,), jnp.float32)
    enter_decay, enter_state = prefix(
        (dev_decay, local_final), "seq", link, (ones_heads, zero_state)
    )
    c_wide = c_blocks.astype(jnp.float32)
    before_block = jnp.concatenate([ones_heads[None], jnp.cumprod(decays, axis=0)[:-1]], axis=0)
    entering = local_enter + before_block[:, :, None, None] * enter_state[None]
    y_state = jnp.exp(cum_decay)[..., None] * jnp.einsum(
        "kqn,khpn->kqhp", c_wide, entering, precision=highest
    )
    y_total = y_intra + y_state + d_skip[:, None] * x_blocks.astype(jnp.float32)
    y_flat = y_total.reshape(tokens_here, heads * HEAD_DIM)
    gated = y_flat * jax.nn.silu(z_local.astype(jnp.float32))
    square_sums = lax.psum(jnp.sum(gated * gated, axis=1), "head")
    normed = (
        gated * lax.rsqrt(square_sums[:, None] / INNER + stability_constant) * norm_gain
    ).astype(jnp.bfloat16)
    last_index = seq_count - 1
    own_final = dev_decay[:, None, None] * enter_state + local_final
    final_state, keep_x, keep_bc = (
        broadcast(own_final, "seq", last_index),
        broadcast(tail_x.astype(jnp.float32), "seq", last_index).astype(tail_x.dtype),
        broadcast(tail_bc.astype(jnp.float32), "seq", last_index).astype(tail_bc.dtype),
    )
    slab_index = jnp.sum(
        jnp.where(owner[0] == seq_index, jnp.arange(seq_count, dtype=jnp.int32), 0)
    )
    ssm_state = take_slab(final_state.reshape(heads, -1), slab_index, seq_count)[None, None]
    conv_x_state = take_slab(keep_x, slab_index, seq_count)[None, None]
    conv_bc_state = take_slab(keep_bc, slab_index, seq_count)[None, None]
    features = lax.all_gather(normed, "head", axis=1, tiled=True)
    out_cols = out_weight.shape[1]
    mixed_sum = add_rows(features, lax.all_gather(out_weight, ("seq", "rep"), axis=0, tiled=True))
    mixed = mixed_sum.astype(jnp.bfloat16).reshape(1, tokens_here, out_cols)
    return (mixed, ssm_state, conv_x_state, conv_bc_state)


def solution(mesh):
    return jax.shard_map(
        local,
        mesh=mesh,
        in_specs=(
            P(("grp", "rep"), None, "seq", None, "head"),
            P(("grp", "rep"), None, "seq", None, "head"),
            P(("grp", "rep"), None, "seq", None, None),
            P(("grp", "rep"), None, "seq", None, "head"),
            P("head"),
            P("head"),
            P("head"),
            P(None, "head"),
            P(),
            P("head"),
            P(("seq", "rep"), "head"),
            P(("grp", "rep")),
            P(("grp", "rep"), None),
        ),
        out_specs=(
            P(("grp", "rep"), "seq", "head"),
            P(("grp", "rep"), "seq", "head", None),
            P(("grp", "rep"), "seq", None, "head"),
            P(("grp", "rep"), "seq", None, None),
        ),
        check_vma=False,
    )
```

profile of v0, /device:TPU:40, one launch (start us, length us, event | category | flops | bytes accessed | tf_op | source)
XLA Modules:
  0.0 892.7 jit_solution(16891518025906551019)
XLA Ops:
  8.1 2.9 pad_maximum_fusion
  10.9 45.8 %all-to-all-start = ((bf16[1,32,1,4,4384]{4,3,2,0,1:T(4,128)(2,1)}), bf16[1,32,1,4,4384]{4,3,2,0,1:T(4,128)(2,1)S(1)}, u32[]{:S(2)}, u32[]{:S(2)}) async-start(bf16[1,32,1,4,4384]{4,3,2,0,1:T(4,128)(2,1)} %pad_maximum_fusion), calls=%async_computation | async-start | bytes 2293760 | tf_op jit(solution)/shard_map/all_to_all | solution.py:25
  57.5 111.5 %all-to-all-done = bf16[1,32,1,4,4384]{4,3,2,0,1:T(4,128)(2,1)S(1)} async-done(((bf16[1,32,1,4,4384]{4,3,2,0,1:T(4,128)(2,1)}), bf16[1,32,1,4,4384]{4,3,2,0,1:T(4,128)(2,1)S(1)}, u32[]{:S(2)}, u32[]{:S(2)}) %all-to-all-start) | async-done | bytes 1122336 | tf_op jit(solution)/shard_map/all_to_all | solution.py:25
  170.6 3.9 collective-permute-start
  174.6 1.9 collective-permute-start.1
  176.7 8.4 collective-permute-done.1
  185.2 2.9 fusion.8
  189.6 58.3 %all-gather = f32[32,1,32]{2,1,0:T(1,128)S(1)} all-gather(f32[1,1,32]{2,1,0:T(1,128)S(1)} %get-tuple-element.155), channel_id=2, replica_groups=mesh['grp'=2,'seq'=32,'head'=4,'rep'=2] {'seq'}, dimensions={0}, use_global_device_ids=true | all-gather | bytes 4224 | tf_op jit(solution)/shard_map/all_gather | solution.py:40
  247.9 310.6 %all-gather.10.cloned.1.call-done = f32[1024,64,128]{2,1,0:T(8,128)} async-done(((f32[32,64,128]{2,1,0:T(8,128)}), f32[1024,64,128]{2,1,0:T(8,128)}) %all-gather.10.cloned.1.call-update) | async-done | bytes 33554448 | tf_op jit(solution)/shard_map/all_gather | solution.py:40
  558.5 48.1 %while.9 = (s32[]{:T(128)}, f32[32,64,128]{2,1,0:T(8,128)S(1)}, s32[]{:T(128)}, f32[32,32]{1,0:T(8,128)S(1)}, f32[32,32,64,128]{3,2,1,0:T(8,128)}, /*index=5*/s32[]{:T(128)}, s32[]{:T(128)}) while((s32[]{:T(128)}, f32[32,64,128]{2,1,0:T(8,128)S(1)}, s32[]{:T(128)}, f32[32,32]{1,0:T(8,128)S(1)}, f32[32,32,64,128]{3,2,1,0:T(8,128)}, ...), condition=%wide.region_2.3_spmd.clone, body=%wide.region_1.2_spmd.clone.sunk | while | flops 1048580 | bytes 3146217 | solution.py:52
  558.5 1.5 fusion.43
  560.1 1.5 fusion.43
  561.6 1.5 fusion.43
  563.1 1.5 fusion.43
  564.6 1.5 fusion.43
  566.1 1.5 fusion.43
  567.6 1.5 fusion.43
  569.1 1.5 fusion.43
  572.1 1.5 fusion.43
  573.6 1.5 fusion.43
  575.1 1.5 fusion.43
  576.6 1.5 fusion.43
  578.1 1.5 fusion.43
  579.6 1.5 fusion.43
  581.1 1.5 fusion.43
  607.8 2.5 reshape_reshape.3
  611.1 2.4 reshape.434
  615.0 3.8 copy.93
  621.6 10.6 %psum.28 = f32[128]{0:T(128)S(1)} all-reduce(f32[128]{0:T(128)S(1)} %get-tuple-element.166), channel_id=1, replica_groups=mesh['grp'=2,'seq'=32,'head'=4,'rep'=2] {'head'}, use_global_device_ids=true, to_apply=%region_4.5 | all-reduce | flops 128 | bytes 1024 | tf_op jit(solution)/shard_map/psum | solution.py:177
  636.4 135.4 %all-reduce = (bf16[3,2048]{0,1:T(8,128)(2,1)S(1)}, bf16[3,256]{1,0:T(4,128)(2,1)S(1)}) all-reduce(f32[3,2048]{0,1:T(8,128)S(1)} %convert_select_fusion, f32[3,256]{1,0:T(4,128)S(1)} %convert_select_fusion.1), channel_id=1, replica_groups=mesh['grp'=2,'seq'=32,'head'=4,'rep'=2] {'seq'}, use_global_device_ids=true, to_apply=%region_7.8 | all-reduce | flops 6912 | bytes 41472 | tf_op jit(solution)/shard_map/psum | solution.py:57
  773.1 104.6 %all-reduce.3.cloned.1.call-done = f32[32,32,256]{2,1,0:T(8,128)} async-done(((f32[32,32,256]{2,1,0:T(8,128)}), f32[32,32,256]{2,1,0:T(8,128)}) %all-reduce.3.cloned.1.call-update) | async-done | bytes 1048592 | tf_op jit(solution)/shard_map/psum | solution.py:57
  879.3 6.0 fusion.4
  (131 shorter events, 39.6 us)
Async XLA Ops:
  8.0 49.4 %copy-start.10 = (f32[32]{0:T(128)S(1)}, f32[32]{0:T(128)}, u32[]{:S(2)}) copy-start(f32[32]{0:T(128)} %param.19) | copy-start | bytes 388
  8.0 49.4 %copy-start.8 = (f32[4,256]{1,0:T(4,128)S(1)}, f32[4,256]{1,0:T(4,128)}, u32[]{:S(2)}) copy-start(f32[4,256]{1,0:T(4,128)} %param.23) | copy-start | bytes 12292
  8.1 49.4 %copy-start.6 = (f32[4,2048]{1,0:T(4,128)S(1)}, f32[4,2048]{1,0:T(4,128)}, u32[]{:S(2)}) copy-start(f32[4,2048]{1,0:T(4,128)} %param.22) | copy-start | bytes 98308
  8.1 161.0 %copy-start.9 = (f32[32]{0:T(128)S(1)}, f32[32]{0:T(128)}, u32[]{:S(2)}) copy-start(f32[32]{0:T(128)} %param.20) | copy-start | bytes 388
  10.9 158.1 %all-to-all-start = ((bf16[1,32,1,4,4384]{4,3,2,0,1:T(4,128)(2,1)}), bf16[1,32,1,4,4384]{4,3,2,0,1:T(4,128)(2,1)S(1)}, u32[]{:S(2)}, u32[]{:S(2)}) async-start(bf16[1,32,1,4,4384]{4,3,2,0,1:T(4,128)(2,1)} %pad_maximum_fusion), calls=%async_computation | async-start | bytes 2293760 | tf_op jit(solution)/shard_map/all_to_all | solution.py:25
  56.7 501.8 %all-gather.10.cloned.1.call-start = ((), (), s32[]{:S(2)}) async-start(), calls=%async_computation.4 | async-start | bytes 34603008 | tf_op jit(solution)/shard_map/all_gather | solution.py:40
  170.3 19.1 %copy-start.1 = (bf16[128,2048]{0,1:T(8,128)(2,1)}, bf16[128,2048]{0,1:T(8,128)(2,1)S(1)}, u32[]{:S(2)}) copy-start(bf16[128,2048]{0,1:T(8,128)(2,1)S(1)} %broadcast_select_fusion) | copy-start | bytes 1572868
  170.6 14.6 %collective-permute-start = (bf16[3,2048]{0,1:T(8,128)(2,1)S(1)}, bf16[3,2048]{0,1:T(8,128)(2,1)S(1)}, u32[]{:S(2)}, u32[]{:S(2)}) collective-permute-start(bf16[3,2048]{0,1:T(8,128)(2,1)S(1)} %slice.77), channel_id=1, source_target_pairs={{0,8},{8,16},{16,24},{24,32},{32,40},{40,48},{48,56},{56,64},{64,7... | collective-permute-start | bytes 36872 | tf_op jit(solution)/shard_map/ppermute | solution.py:35
  174.6 10.5 %collective-permute-start.1 = (bf16[3,256]{1,0:T(4,128)(2,1)S(1)}, bf16[3,256]{1,0:T(4,128)(2,1)S(1)}, u32[]{:S(2)}, u32[]{:S(2)}) collective-permute-start(bf16[3,256]{1,0:T(4,128)(2,1)S(1)} %slice.82), channel_id=1, source_target_pairs={{0,8},{8,16},{16,24},{24,32},{32,40},{40,48},{48,56},{56,64},{64,7... | collective-permute-start | bytes 4616 | tf_op jit(solution)/shard_map/ppermute | solution.py:35
  189.5 688.2 %all-reduce.3.cloned.1.call-start = ((), (), s32[]{:S(2)}) async-start(), calls=%async_computation.3 | async-start | bytes 2097152 | tf_op jit(solution)/shard_map/psum | solution.py:57
  558.5 48.1 %copy-start = (f32[32,64,128]{2,1,0:T(8,128)S(1)}, f32[32,64,128]{2,1,0:T(8,128)}, u32[]{:S(2)}) copy-start(f32[32,64,128]{2,1,0:T(8,128)} %convolution_add_fusion) | copy-start | bytes 3145732
  610.4 268.9 %all-gather.8.cloned.1.call-start = ((), (), s32[]{:S(2)}) async-start(), calls=%async_computation.2 | async-start | bytes 8519680 | tf_op jit(solution)/shard_map/all_gather | solution.py:196
  611.0 268.2 %all-gather.6.cloned.1.call-start = ((), (), s32[]{:S(2)}) async-start(), calls=%async_computation.1 | async-start | bytes 2621440 | tf_op jit(solution)/shard_map/all_gather | solution.py:194
  614.9 3.9 copy-start.3
  618.8 1.1 copy-start.11
  619.1 1.2 copy-start.4
  619.2 1.4 copy-start.5
  620.5 11.8 %copy-start.7 = (f32[2048]{0:T(1024)S(1)}, f32[2048]{0:T(1024)}, u32[]{:S(2)}) copy-start(f32[2048]{0:T(1024)} %param.24) | copy-start | bytes 24580
  621.6 11.9 %copy-start.12 = (s32[1,32]{1,0:T(1,128)S(1)}, s32[1,32]{1,0:T(1,128)}, u32[]{:S(2)}) copy-start(s32[1,32]{1,0:T(1,128)} %param.27) | copy-start | bytes 388
  621.6 14.5 %copy-start.2 = (bf16[128,2048]{0,1:T(8,128)(2,1)S(1)}, bf16[128,2048]{0,1:T(8,128)(2,1)}, u32[]{:S(2)}) copy-start(bf16[128,2048]{0,1:T(8,128)(2,1)} %copy-done.1) | copy-start | bytes 1572868
Sparse Core Ops, SparseCore 0:
  189.6 368.8 all-gather.9
  610.5 267.1 all-reduce.2
Sparse Core Ops, SparseCore 1:
  613.0 144.6 all-gather.7
  759.7 38.2 all-gather.5
where the time goes:
time: 895 us; the launch traced here: 893 us
  waiting for transfers between devices  536 us (60%)
  blocking collectives  204 us (23%)
  other arithmetic  56.9 us (6%)
  starting transfers between devices  51.9 us (6%)
  between operations  18.5 us (2%)
  local copies, waits for them, and re-layouts  15.2 us (2%)
  matrix products  9.14 us (1%)
    all_gather x1, waiting for transfers between devices, prefix(): everything = jax.tree.map(lambda part: lax.all_gather(part, axis), value)  311 us
    psum x1, blocking collectives, broadcast(): return lax.psum(block, axis)  135 us
    all_to_all x1, waiting for transfers between devices, side_by_side(): lax.all_to_all(both, axis, split_axis=split_dim, concat_axis=concat_dim,...  112 us
    psum x1, waiting for transfers between devices, broadcast(): return lax.psum(block, axis)  105 us
    all_gather x1, blocking collectives, prefix(): everything = jax.tree.map(lambda part: lax.all_gather(part, axis), value)  58.3 us
    select_n x32, other arithmetic, lap(): return jax.tree.map(lambda a, b: jnp.where(reached, a, b), new, before)  46.9 us
    all_to_all x1, starting transfers between devices, side_by_side(): lax.all_to_all(both, axis, split_axis=split_dim, concat_axis=concat_dim,...  45.8 us
  transfers between devices with their start and end apart: 7, of which 4 were waited for; matrix products, arithmetic and copies ran while one was open for 2% of the time, Pallas kernels for 0%

commit v1 on v0

v1 whole, which is shorter than its diff:
```python
import functools

import jax
import jax.numpy as jnp
from jax import lax
from jax.experimental import pallas as pl
from jax.experimental.pallas import tpu as pltpu
from jax.sharding import PartitionSpec as P

HEAD_DIM = 64
NSTATE = 128
KCONV = 4
EPS = 1e-05
LANES = 128
EXTRA = 8

highest = lax.Precision.HIGHEST
f32, bf16 = jnp.float32, jnp.bfloat16


def silu(v):
    return v * (1.0 / (1.0 + jnp.exp(-v)))


def softplus(v):
    return jnp.maximum(v, 0.0) + jnp.log1p(jnp.exp(-jnp.abs(v)))


def head_kernel(
    start_ref, par_ref, wbc_ref, x_ref, dt_ref, bc_ref,
    y_ref, hi_ref, lo_ref,
    cum_ref, w_ref, step_ref, extx_ref, extbc_ref, bc_conv_ref, s_ref,
):
    pairs, span, _ = x_ref.shape
    blocks = 2 * pairs
    start = start_ref[0]
    row = lax.broadcasted_iota(jnp.int32, (span, LANES), 0)
    lane = lax.broadcasted_iota(jnp.int32, (span, LANES), 1)
    odd = lane >= HEAD_DIM

    pos = lax.broadcasted_iota(jnp.int32, (blocks, span), 0) * span + lax.broadcasted_iota(
        jnp.int32, (blocks, span), 1
    )
    live = (pos >= start).astype(f32)
    step = softplus(dt_ref[...].astype(f32) + par_ref[5:6, :]) * live
    log_decay = -par_ref[4:5, :] * step
    upto = (row <= lane).astype(f32)
    cum = jnp.dot(log_decay, upto, precision=highest, preferred_element_type=f32)
    cum_ref[...] = cum
    w_ref[...] = jnp.exp(cum[:, span - 1 : span] - cum) * step
    step_ref[...] = step

    extx_ref[0:8, :] = jnp.zeros((8, LANES), f32)
    extbc_ref[0:8, :] = jnp.zeros((8, 2 * NSTATE), f32)
    s_ref[...] = jnp.zeros(s_ref.shape, f32)
    causal = row >= lane
    low8 = lax.broadcasted_iota(jnp.int32, (8, LANES), 1) >= HEAD_DIM

    def pair(i, carry):
        base = i * (2 * span)
        live_x = (base + jnp.where(odd, span, 0) + row) >= start
        xf = jnp.where(live_x, x_ref[i].astype(f32), 0.0)
        last = pltpu.roll(xf[span - 8 :, :], HEAD_DIM, 1)
        extx_ref[0:8, :] = jnp.where(low8, last, extx_ref[0:8, :])
        extx_ref[8 : 8 + span, :] = xf
        acc = jnp.zeros((span, LANES), f32)
        for k in range(KCONV):
            acc = acc + par_ref[k : k + 1, :] * extx_ref[pl.ds(8 - (KCONV - 1) + k, span), :]
        extx_ref[0:8, :] = last
        xc = silu(acc).astype(bf16)
        xcf = xc.astype(f32)

        rows2 = lax.broadcasted_iota(jnp.int32, (2 * span, 2 * NSTATE), 0)
        bcf = jnp.where(base + rows2 >= start, bc_ref[i].astype(f32), 0.0)
        extbc_ref[8 : 8 + 2 * span, :] = bcf
        acc2 = jnp.zeros((2 * span, 2 * NSTATE), f32)
        for k in range(KCONV):
            acc2 = acc2 + wbc_ref[k : k + 1, :] * extbc_ref[pl.ds(8 - (KCONV - 1) + k, 2 * span), :]
        extbc_ref[0:8, :] = bcf[2 * span - 8 :, :]
        bc_conv_ref[...] = silu(acc2).astype(bf16)

        state = s_ref[...]
        ys, ecs, wcs, decays, bs, cs = [], [], [], [], [], []
        for h in range(2):
            c = 2 * i + h
            b_blk = bc_conv_ref[h * span : (h + 1) * span, 0:NSTATE]
            c_blk = bc_conv_ref[h * span : (h + 1) * span, NSTATE : 2 * NSTATE]
            cum_row = cum_ref[pl.ds(c, 1), :]
            cum_b = jnp.broadcast_to(cum_row, (span, span))
            cum_c = cum_b.T
            w_c = jnp.broadcast_to(w_ref[pl.ds(c, 1), :], (span, span)).T
            seg = jnp.exp(jnp.where(causal, cum_c - cum_b, -1e30))
            scores = lax.dot_general(
                c_blk, b_blk, (((1,), (1,)), ((), ())), preferred_element_type=f32
            )
            mix = (scores * seg * step_ref[pl.ds(c, 1), :]).astype(bf16)
            ys.append(jnp.dot(mix, xc, preferred_element_type=f32))
            e_c = jnp.exp(cum_c)
            ecs.append(e_c)
            wcs.append(w_c)
            decays.append(e_c[span - 1 : span, :])
            bs.append(b_blk)
            cs.append(c_blk)
        scaled = (jnp.where(odd, wcs[1], wcs[0]) * xcf).astype(bf16)
        adds = [
            lax.dot_general(b, scaled, (((0,), (0,)), ((), ())), preferred_element_type=f32)
            for b in bs
        ]
        after_even = decays[0] * state + adds[0]
        entering = jnp.where(odd, pltpu.roll(after_even, HEAD_DIM, 1), state)
        ent_hi = entering.astype(bf16)
        ent_lo = (entering - ent_hi.astype(f32)).astype(bf16)
        outs = []
        for h in range(2):
            from_state = jnp.dot(cs[h], ent_hi, preferred_element_type=f32) + jnp.dot(
                cs[h], ent_lo, preferred_element_type=f32
            )
            outs.append(ys[h] + ecs[h] * from_state)
        y = jnp.where(odd, outs[1], outs[0]) + par_ref[6:7, :] * xcf
        y_ref[i] = y.astype(bf16)
        after_odd = decays[1] * entering + adds[1]
        s_ref[...] = pltpu.roll(after_odd, HEAD_DIM, 1)
        return carry

    lax.fori_loop(0, pairs, pair, 0)
    final = s_ref[...].T[0:HEAD_DIM, :]
    hi = final.astype(bf16)
    hi_ref[...] = hi
    lo_ref[...] = (final - hi.astype(f32)).astype(bf16)


def run_head(start, par, wbc, x, dt, bc):
    pairs, span, _ = x.shape
    vmem = pl.BlockSpec(memory_space=pltpu.VMEM)
    return pl.pallas_call(
        head_kernel,
        out_shape=(
            jax.ShapeDtypeStruct((pairs, span, LANES), bf16),
            jax.ShapeDtypeStruct((HEAD_DIM, NSTATE), bf16),
            jax.ShapeDtypeStruct((HEAD_DIM, NSTATE), bf16),
        ),
        in_specs=[pl.BlockSpec(memory_space=pltpu.SMEM)] + [vmem] * 5,
        out_specs=(vmem, vmem, vmem),
        scratch_shapes=[
            pltpu.VMEM((2 * pairs, span), f32),
            pltpu.VMEM((2 * pairs, span), f32),
            pltpu.VMEM((2 * pairs, span), f32),
            pltpu.VMEM((8 + span, LANES), f32),
            pltpu.VMEM((8 + 2 * span, 2 * NSTATE), f32),
            pltpu.VMEM((2 * span, 2 * NSTATE), bf16),
            pltpu.VMEM((NSTATE, LANES), f32),
        ],
        compiler_params=pltpu.CompilerParams(vmem_limit_bytes=32 * 1024 * 1024),
        cost_estimate=pl.CostEstimate(flops=1_000_000_000, bytes_accessed=5_000_000, transcendentals=3_000_000),
        name="head_scan",
    )(start, par, wbc, x, dt, bc)


def exchange(value, axis):
    return lax.all_to_all(value, axis, split_axis=0, concat_axis=0, tiled=True)


def local(
    x_proj, gate_proj, bc_proj, dt_proj, a_rate, dt_bias, d_skip,
    conv_x_weight, conv_bc_weight, norm_gain, out_weight, request_first_position, owner,
):
    _, blocks, _, sub, width = x_proj.shape
    n = lax.axis_size("seq")
    me = lax.axis_index("seq")
    pairs = blocks // 2
    rows = pairs * sub
    span = n * sub
    inner = width * lax.axis_size("head")

    x_send = x_proj.reshape(pairs, 2, sub, n, HEAD_DIM).transpose(3, 0, 2, 1, 4).reshape(n, rows, LANES)
    dt_send = dt_proj.reshape(pairs, 2, sub, n).transpose(3, 1, 0, 2).reshape(n, 2 * rows // LANES, LANES)
    pad = jnp.zeros((n, EXTRA - dt_send.shape[1], LANES), bf16)
    got = exchange(jnp.concatenate([x_send, dt_send, pad], axis=1), "seq")
    x_head = got[:, :rows].reshape(n, pairs, sub, LANES).transpose(1, 0, 2, 3).reshape(pairs, span, LANES)
    dt_head = (
        got[:, rows : rows + dt_send.shape[1]]
        .reshape(n, 2, pairs, sub).transpose(2, 1, 0, 3).reshape(blocks, span)
    )
    bc_all = lax.all_gather(bc_proj.reshape(blocks, sub, 2 * NSTATE), "seq")
    bc_head = bc_all.transpose(1, 0, 2, 3).reshape(pairs, 2 * span, 2 * NSTATE)

    def lanes(v):
        return jnp.broadcast_to(v, (1, LANES))

    w_mine = lax.dynamic_slice_in_dim(conv_x_weight, me * HEAD_DIM, HEAD_DIM, 1)
    par = jnp.concatenate(
        [jnp.concatenate([w_mine, w_mine], axis=1)]
        + [lanes(lax.dynamic_index_in_dim(v, me, 0)) for v in (a_rate, dt_bias, d_skip)]
        + [jnp.zeros((1, LANES), f32)],
        axis=0,
    )
    y, hi, lo = run_head(request_first_position, par, conv_bc_weight, x_head, dt_head, bc_head)

    slab_of = jnp.sum(
        jnp.where(owner[0][None, :] == jnp.arange(n, dtype=jnp.int32)[:, None],
                  jnp.arange(n, dtype=jnp.int32)[None, :], 0),
        axis=1,
    )
    per = HEAD_DIM // n * NSTATE // LANES if HEAD_DIM >= n else 1
    keep = KCONV - 1
    live_tail = (
        blocks * span - keep + jnp.arange(keep, dtype=jnp.int32) >= request_first_position[0]
    )
    tail_x = jnp.where(live_tail[:, None], x_head[pairs - 1, span - keep :], jnp.zeros((), bf16))
    y_send = y.reshape(pairs, n, sub, LANES).transpose(1, 0, 2, 3).reshape(n, rows, LANES)
    slabs_hi = jnp.take(hi.reshape(n, per, LANES), slab_of, axis=0)
    slabs_lo = jnp.take(lo.reshape(n, per, LANES), slab_of, axis=0)
    used = 2 * per + keep
    extra_rows = -(-used // 8) * 8
    back = exchange(
        jnp.concatenate(
            [
                y_send,
                slabs_hi,
                slabs_lo,
                jnp.broadcast_to(tail_x[None], (n, keep, LANES)),
                jnp.zeros((n, extra_rows - used, LANES), bf16),
            ],
            axis=1,
        ),
        "seq",
    )
    y_mine = (
        back[:, :rows].reshape(n, pairs, sub, 2, HEAD_DIM).transpose(1, 3, 2, 0, 4)
        .reshape(blocks * sub, width)
    )
    state_mine = back[:, rows : rows + per].astype(f32) + back[:, rows + per : rows + 2 * per].astype(f32)
    ssm_state = state_mine.reshape(1, 1, n, per * LANES)
    my_slab = slab_of[me]
    conv_x_state = lax.dynamic_index_in_dim(
        back[:, rows + 2 * per : rows + used, HEAD_DIM:], my_slab, 0
    )[None]
    tail_bc = jnp.where(
        live_tail[:, None], bc_head[pairs - 1, 2 * span - keep :], jnp.zeros((), bf16)
    )
    conv_bc_state = lax.dynamic_index_in_dim(
        tail_bc.reshape(keep, n, -1), my_slab, axis=1, keepdims=False
    )[None, None]

    gate = gate_proj.reshape(blocks * sub, width).astype(f32)
    gated = y_mine.astype(f32) * jax.nn.silu(gate)
    squares = lax.psum(jnp.sum(gated * gated, axis=1), "head")
    normed = (gated * lax.rsqrt(squares[:, None] / inner + EPS) * norm_gain).astype(bf16)
    features = lax.all_gather(normed, "head", axis=1, tiled=True)
    weight = lax.all_gather(out_weight, ("seq", "rep"), axis=0, tiled=True)
    mixed = jnp.dot(features, weight, preferred_element_type=f32).astype(bf16)
    cols = mixed.shape[1]
    mixed = exchange(mixed.reshape(blocks, sub, cols), "seq").reshape(1, span, cols)
    return (mixed, ssm_state, conv_x_state, conv_bc_state)


def solution(mesh):
    return jax.shard_map(
        local,
        mesh=mesh,
        in_specs=(
            P(("grp", "rep"), None, "seq", None, "head"),
            P(("grp", "rep"), None, "seq", None, "head"),
            P(("grp", "rep"), None, "seq", None, None),
            P(("grp", "rep"), None, "seq", None, "head"),
            P("head"),
            P("head"),
            P("head"),
            P(None, "head"),
            P(),
            P("head"),
            P(("seq", "rep"), "head"),
            P(("grp", "rep")),
            P(("grp", "rep"), None),
        ),
        out_specs=(
            P(("grp", "rep"), "seq", "head"),
            P(("grp", "rep"), "seq", "head", None),
            P(("grp", "rep"), "seq", None, "head"),
            P(("grp", "rep"), "seq", None, None),
        ),
        check_vma=False,
    )
```

time: 895 us -> 555 us (0.62)
  blocking collectives: 204 us -> 11.5 us
  waiting for transfers between devices: 536 us -> 389 us
  other arithmetic: 56.9 us -> 9.79 us
  local copies, waits for them, and re-layouts: 15.2 us -> 35.9 us
  starting transfers between devices: 51.9 us -> 71.7 us
  Pallas kernels: 0 us -> 13 us
    psum x2 -> x1, blocking collectives: 146 us -> 11.5 us  [local(): squares = lax.psum(jnp.sum(gated * gated, axis=1), 'head')]
    psum x1 -> x0, waiting for transfers between devices: 105 us -> none  [broadcast(): return lax.psum(block, axis)]
    all_gather x1 -> x0, blocking collectives: 58.3 us -> none  [prefix(): everything = jax.tree.map(lambda part: lax.all_gather(part, axis), value)]
    select_n x37 -> x3, other arithmetic: 48.4 us -> 0.19 us  [the longest x1 0.1 us: local(): slabs_lo = jnp.take(lo.reshape(n, per, LANES), slab_of, axis=0)]
    all_to_all x1 -> x3, waiting for transfers between devices: 112 us -> 72.4 us  [exchange(): return lax.all_to_all(value, axis, split_axis=0, concat_axis=0, tiled=True)]
    all_gather x1, waiting for transfers between devices: 0.01 us -> 26.4 us  [local(): features = lax.all_gather(normed, 'head', axis=1, tiled=True)]
    all_to_all x1 -> x3, starting transfers between devices: 45.8 us -> 71.3 us  [exchange(): return lax.all_to_all(value, axis, split_axis=0, concat_axis=0, tiled=True)]
    all_gather x2, waiting for transfers between devices: 311 us -> 290 us  [the longest x1 146 us: local(): bc_all = lax.all_gather(bc_proj.reshape(blocks, sub, 2 * NSTATE), 'seq')]
  transfers between devices with their start and end apart: 7 -> 6, of which waited for: 4 -> 5; matrix products, arithmetic and copies ran while one was open for 2% -> 3% of each run, Pallas kernels for 0% -> 0%
where the time goes in v1:
time: 555 us; the launch traced here: 553 us
  waiting for transfers between devices  389 us (70%)
  starting transfers between devices  71.7 us (13%)
  local copies, waits for them, and re-layouts  35.9 us (6%)
  between operations  16.8 us (3%)
  Pallas kernels  13 us (2%)
  blocking collectives  11.5 us (2%)
  other arithmetic  9.79 us (2%)
    all_gather x1, waiting for transfers between devices, local(): bc_all = lax.all_gather(bc_proj.reshape(blocks, sub, 2 * NSTATE), 'seq')  146 us
    all_gather x1, waiting for transfers between devices, local(): weight = lax.all_gather(out_weight, ('seq', 'rep'), axis=0, tiled=True)  144 us
    all_to_all x3, waiting for transfers between devices, exchange(): return lax.all_to_all(value, axis, split_axis=0, concat_axis=0, tiled=True)  72.4 us
    all_to_all x3, starting transfers between devices, exchange(): return lax.all_to_all(value, axis, split_axis=0, concat_axis=0, tiled=True)  71.3 us
    all_gather x1, waiting for transfers between devices, local(): features = lax.all_gather(normed, 'head', axis=1, tiled=True)  26.4 us
    pallas_call x1, Pallas kernels, run_head(): pl.pallas_call(head_kernel, out_shape=(jax.ShapeDtypeStruct((pairs, span,...  13 us
    psum x1, blocking collectives, local(): squares = lax.psum(jnp.sum(gated * gated, axis=1), 'head')  11.5 us
  transfers between devices with their start and end apart: 6, of which 5 were waited for; matrix products, arithmetic and copies ran while one was open for 3% of the time, Pallas kernels for 0%

profile of v1, /device:TPU:40, one launch (start us, length us, event | category | flops | bytes accessed | tf_op | source)
XLA Modules:
  0.0 553.1 jit_solution(11687252360655227128)
XLA Ops:
  7.2 2.0 reshape.110
  9.2 1.1 copy.81
  11.1 1.0 maximum_maximum_fusion
  12.1 45.8 %all-to-all-start = ((bf16[32,72,128]{2,1,0:T(8,128)(2,1)}), bf16[32,72,128]{2,1,0:T(8,128)(2,1)S(1)}, u32[]{:S(2)}, u32[]{:S(2)}) async-start(bf16[32,72,128]{2,1,0:T(8,128)(2,1)} %maximum_maximum_fusion), calls=%async_computation | async-start | bytes 1179648 | tf_op jit(solution)/shard_map/all_to_all | solution.py:160
  61.2 0.6 broadcast_in_dim.89
  61.9 0.6 broadcast_in_dim.90
  63.3 145.5 %all-gather.9.cloned.1.call-done = bf16[32,32,1,4,256]{4,1,3,2,0:T(8,128)(2,1)} async-done(((bf16[1,32,1,4,256]{4,1,3,2,0:T(8,128)(2,1)}), bf16[32,32,1,4,256]{4,1,3,2,0:T(8,128)(2,1)}) %all-gather.9.cloned.1.call-update) | async-done | bytes 2097168 | tf_op jit(solution)/shard_map/all_gather | solution.py:184
  208.9 4.5 copy.66
  213.4 2.5 reshape.118.bc_ref
  217.5 13.0 %head_scan.1 = (bf16[16,128,128]{2,1,0:T(8,128)(2,1)S(1)}, bf16[64,128]{1,0:T(8,128)(2,1)S(1)}, bf16[64,128]{1,0:T(8,128)(2,1)S(1)}) custom-call(s32[1]{0:T(128)} %copy.87.start_ref, f32[8,128]{1,0:T(8,128)S(1)} %concatenate.13.par_ref, f32[4,256]{1,0:T(4,128)S(1)} %copy-done.1, bf16[16,128,128]{2,1,0:T(8,128)(2,1)S(1)} %bitcast.48, ...), custom_call_target="tpu_custom_call" | custom-call | flops 1000000000 | bytes 5000000 | tf_op jit(solution)/shard_map/head_scan/pallas_call | solution.py:135
  232.1 1.1 copy.70
  233.2 13.4 %all-to-all-start.1 = ((bf16[32,72,128]{2,1,0:T(8,128)(2,1)}), bf16[32,72,128]{2,1,0:T(8,128)(2,1)}, u32[]{:S(2)}, u32[]{:S(2)}) async-start(bf16[32,72,128]{2,1,0:T(8,128)(2,1)} %copy.70), calls=%async_computation.1 | async-start | bytes 1179648 | tf_op jit(solution)/shard_map/all_to_all | solution.py:160
  246.9 2.1 reshape.128
  248.9 1.1 reshape.127
  250.0 47.6 %all-to-all-done.1 = bf16[32,72,128]{2,1,0:T(8,128)(2,1)} async-done(((bf16[32,72,128]{2,1,0:T(8,128)(2,1)}), bf16[32,72,128]{2,1,0:T(8,128)(2,1)}, u32[]{:S(2)}, u32[]{:S(2)}) %all-to-all-start.1) | async-done | bytes 589856 | tf_op jit(solution)/shard_map/all_to_all | solution.py:160
  297.5 1.1 slice_convert_fusion
  298.7 2.5 reshape.130
  301.2 4.2 copy.80
  305.4 2.1 reshape.126
  307.5 3.8 multiply_reduce_fusion
  311.4 11.5 %psum.7 = f32[128]{0:T(128)S(1)} all-reduce(f32[128]{0:T(128)S(1)} %reduce_sum.22), channel_id=1, replica_groups=mesh['grp'=2,'seq'=32,'head'=4,'rep'=2] {'head'}, use_global_device_ids=true, to_apply=%region_2.4 | all-reduce | flops 128 | bytes 1024 | tf_op jit(solution)/shard_map/psum | solution.py:247
  322.9 2.4 multiply_convert_fusion
  325.4 0.7 all-gather.7.cloned.1.call-update
  326.1 26.4 %all-gather.5.cloned.1.call-done = bf16[128,8192]{1,0:T(8,128)(2,1)} async-done(((bf16[128,2048]{1,0:T(8,128)(2,1)}), bf16[128,8192]{1,0:T(8,128)(2,1)}) %all-gather.5.cloned.1.call-update) | async-done | bytes 2097168 | tf_op jit(solution)/shard_map/all_gather | solution.py:249
  352.5 144.0 %all-gather.7.cloned.1.call-done = bf16[8192,512]{1,0:T(8,128)(2,1)} async-done(((bf16[128,512]{1,0:T(8,128)(2,1)}), bf16[8192,512]{1,0:T(8,128)(2,1)}) %all-gather.7.cloned.1.call-update) | async-done | bytes 8388624 | tf_op jit(solution)/shard_map/all_gather | solution.py:250
  496.5 5.3 convolution_convert_fusion
  501.8 0.7 reshape.123
  502.5 12.1 %all-to-all-start.2 = ((bf16[32,4,512]{2,1,0:T(4,128)(2,1)}), bf16[32,4,512]{2,1,0:T(4,128)(2,1)S(1)}, u32[]{:S(2)}, u32[]{:S(2)}) async-start(bf16[32,4,512]{2,1,0:T(4,128)(2,1)} %reshape.123), calls=%async_computation.2 | async-start | bytes 262144 | tf_op jit(solution)/shard_map/all_to_all | solution.py:160
  517.9 0.9 convert_add_fusion
  519.5 0.9 slice.42
  521.0 24.8 %all-to-all-done.2 = bf16[32,4,512]{2,1,0:T(4,128)(2,1)S(1)} async-done(((bf16[32,4,512]{2,1,0:T(4,128)(2,1)}), bf16[32,4,512]{2,1,0:T(4,128)(2,1)S(1)}, u32[]{:S(2)}, u32[]{:S(2)}) %all-to-all-start.2) | async-done | bytes 131104 | tf_op jit(solution)/shard_map/all_to_all | solution.py:160
  545.9 0.7 reshape.124
  (71 shorter events, 10.2 us)
Async XLA Ops:
  7.2 53.9 %copy-start = (f32[4,2048]{1,0:T(4,128)S(1)}, f32[4,2048]{1,0:T(4,128)}, u32[]{:S(2)}) copy-start(f32[4,2048]{1,0:T(4,128)} %param.22) | copy-start | bytes 98308
  9.2 1.6 copy-start.4
  10.3 47.6 %copy-start.3 = (bf16[1,32,1,4,256]{4,3,2,1,0:T(4,128)(2,1)S(1)}, bf16[1,32,1,4,256]{4,3,2,1,0:T(4,128)(2,1)}, u32[]{:S(2)}) copy-start(bf16[1,32,1,4,256]{4,3,2,1,0:T(4,128)(2,1)} %param.17) | copy-start | bytes 196612
  10.3 48.3 %copy-start.6 = (f32[32]{0:T(128)S(1)}, f32[32]{0:T(128)}, u32[]{:S(2)}) copy-start(f32[32]{0:T(128)} %param.19) | copy-start | bytes 388
  10.3 48.9 %copy-start.7 = (f32[32]{0:T(128)S(1)}, f32[32]{0:T(128)}, u32[]{:S(2)}) copy-start(f32[32]{0:T(128)} %param.20) | copy-start | bytes 388
  10.3 49.5 %copy-start.8 = (f32[32]{0:T(128)S(1)}, f32[32]{0:T(128)}, u32[]{:S(2)}) copy-start(f32[32]{0:T(128)} %param.21) | copy-start | bytes 388
  10.4 52.8 %copy-start.9 = (s32[1,32]{1,0:T(1,128)S(1)}, s32[1,32]{1,0:T(1,128)}, u32[]{:S(2)}) copy-start(s32[1,32]{1,0:T(1,128)} %param.27) | copy-start | bytes 388
  12.1 203.9 %all-to-all-start = ((bf16[32,72,128]{2,1,0:T(8,128)(2,1)}), bf16[32,72,128]{2,1,0:T(8,128)(2,1)S(1)}, u32[]{:S(2)}, u32[]{:S(2)}) async-start(bf16[32,72,128]{2,1,0:T(8,128)(2,1)} %maximum_maximum_fusion), calls=%async_computation | async-start | bytes 1179648 | tf_op jit(solution)/shard_map/all_to_all | solution.py:160
  57.9 151.0 %all-gather.9.cloned.1.call-start = ((), (), s32[]{:S(2)}) async-start(), calls=%async_computation.5 | async-start | bytes 2162688 | tf_op jit(solution)/shard_map/all_gather | solution.py:184
  215.9 1.5 copy-start.1
  231.8 15.0 %copy-start.2 = (bf16[1,32,1,4,2048]{4,3,2,1,0:T(4,128)(2,1)S(1)}, bf16[1,32,1,4,2048]{4,3,2,1,0:T(4,128)(2,1)}, u32[]{:S(2)}) copy-start(bf16[1,32,1,4,2048]{4,3,2,1,0:T(4,128)(2,1)} %param.16) | copy-start | bytes 1572868
  233.2 64.4 %all-to-all-start.1 = ((bf16[32,72,128]{2,1,0:T(8,128)(2,1)}), bf16[32,72,128]{2,1,0:T(8,128)(2,1)}, u32[]{:S(2)}, u32[]{:S(2)}) async-start(bf16[32,72,128]{2,1,0:T(8,128)(2,1)} %copy.70), calls=%async_computation.1 | async-start | bytes 1179648 | tf_op jit(solution)/shard_map/all_to_all | solution.py:160
  246.6 105.9 %all-gather.5.cloned.1.call-start = ((), (), s32[]{:S(2)}) async-start(), calls=%async_computation.3 | async-start | bytes 2621440 | tf_op jit(solution)/shard_map/all_gather | solution.py:249
  307.4 15.4 %copy-start.5 = (f32[2048]{0:T(1024)S(1)}, f32[2048]{0:T(1024)}, u32[]{:S(2)}) copy-start(f32[2048]{0:T(1024)} %param.24) | copy-start | bytes 24580
  325.3 171.2 %all-gather.7.cloned.1.call-start = ((), (), s32[]{:S(2)}) async-start(), calls=%async_computation.4 | async-start | bytes 8519680 | tf_op jit(solution)/shard_map/all_gather | solution.py:250
  502.5 43.4 %all-to-all-start.2 = ((bf16[32,4,512]{2,1,0:T(4,128)(2,1)}), bf16[32,4,512]{2,1,0:T(4,128)(2,1)S(1)}, u32[]{:S(2)}, u32[]{:S(2)}) async-start(bf16[32,4,512]{2,1,0:T(4,128)(2,1)} %reshape.123), calls=%async_computation.2 | async-start | bytes 262144 | tf_op jit(solution)/shard_map/all_to_all | solution.py:160
Sparse Core Ops, SparseCore 0:
  61.4 147.4 all-gather.8
  325.4 27.0 all-gather.4
  354.6 141.8 all-gather.6

commit v2 on v1

v2 whole, which is shorter than its diff:
```python
import functools

import jax
import jax.numpy as jnp
from jax import lax
from jax.experimental import pallas as pl
from jax.experimental.pallas import tpu as pltpu
from jax.sharding import PartitionSpec as P

HEAD_DIM = 64
NSTATE = 128
KCONV = 4
EPS = 1e-05
LANES = 128
MESH = pl.DeviceIdType.MESH
VM = pl.BlockSpec(memory_space=pltpu.VMEM)
ANY = pl.BlockSpec(memory_space=pl.ANY)

highest = lax.Precision.HIGHEST
f32, bf16 = jnp.float32, jnp.bfloat16


def silu(v):
    return v * (1.0 / (1.0 + jnp.exp(-v)))


def softplus(v):
    return jnp.maximum(v, 0.0) + jnp.log1p(jnp.exp(-jnp.abs(v)))


def copy_to(src, dst, send_sem, recv_sem, device):
    return pltpu.make_async_remote_copy(
        src_ref=src, dst_ref=dst, send_sem=send_sem, recv_sem=recv_sem,
        device_id=device, device_id_type=MESH,
    )


def arrived(region, sem, device):
    copy_to(region, region, sem, sem, device).wait_recv()


def sent(region, sem, device):
    copy_to(region, region, sem, sem, device).wait_send()


def greet():
    barrier = pltpu.get_barrier_semaphore()
    total = 0
    for axis in ("seq", "head"):
        size, here = lax.axis_size(axis), lax.axis_index(axis)

        def hello(k, carry):
            pl.semaphore_signal(
                barrier, inc=1, device_id={axis: lax.rem(here + k, size)}, device_id_type=MESH
            )
            return carry

        lax.fori_loop(1, size, hello, 0)
        total += size - 1
    pl.semaphore_wait(barrier, total)


def offset_of(k):
    half = lax.div(k + 1, 2)
    return jnp.where(lax.rem(k, 2) == 1, half, -half)


def swap_halves(a, b):
    low = lax.broadcasted_iota(jnp.int32, a.shape, 1) < HEAD_DIM
    return (
        jnp.where(low, a, pltpu.roll(b, HEAD_DIM, 1)),
        jnp.where(low, pltpu.roll(a, HEAD_DIM, 1), b),
    )


def in_kernel(
    x_ref, bc_ref, dt_ref, xg_ref, dtg_ref, bcg_ref,
    xs, x_send, x_recv, dt_send, dt_recv, ring_send, ring_recv, side_send, side_recv,
):
    pairs, _, sub, _ = x_ref.shape
    n, quarters = lax.axis_size("seq"), lax.axis_size("head")
    me, g = lax.axis_index("seq"), lax.axis_index("head")
    share = bc_ref.shape[0] // quarters
    right, left = lax.rem(me + 1, n), lax.rem(me + n - 1, n)
    sibling = me + 1 - 2 * lax.rem(me, 2)
    my_pair = lax.div(me, 2)
    mine = bc_ref.at[pl.ds(g * share, share)]

    def slot(owner):
        return bcg_ref.at[pl.ds(g * share, share), owner]

    greet()

    def ring(src, owner, step, way):
        copy_to(
            src, slot(owner), ring_send.at[way, step], ring_recv.at[way, step],
            {"seq": right if way == 0 else left},
        ).start()

    def aside(src, owner):
        for k in range(1, quarters):
            copy_to(
                src, slot(owner), side_send, side_recv.at[k - 1],
                {"head": lax.rem(g + k, quarters)},
            ).start()

    ring(mine, me, 0, 0)
    ring(mine, me, 0, 1)
    bcg_ref[pl.ds(g * share, share), me] = bc_ref[pl.ds(g * share, share)]
    aside(mine, me)

    def dt_out(k, carry):
        to = lax.rem(me + offset_of(k) + n, n)
        copy_to(dt_ref.at[to], dtg_ref.at[me], dt_send, dt_recv, {"seq": to}).start()
        return carry

    lax.fori_loop(1, n, dt_out, 0)
    dtg_ref[me] = dt_ref[me]

    def pack(p):
        cols = pl.ds(pl.multiple_of(p * LANES, LANES), LANES)
        even = x_ref[:, 0, :, cols].reshape(pairs * sub, LANES).astype(f32)
        odd = x_ref[:, 1, :, cols].reshape(pairs * sub, LANES).astype(f32)
        first, second = swap_halves(even, odd)
        xs[2 * p] = first.astype(bf16).reshape(pairs, sub, LANES)
        xs[2 * p + 1] = second.astype(bf16).reshape(pairs, sub, LANES)

    def send_x(to):
        copy_to(xs.at[to], xg_ref.at[:, me], x_send, x_recv, {"seq": to}).start()

    def pair_at(k):
        return lax.rem(my_pair + offset_of(k) + pairs, pairs)

    def take(owner, step, way):
        arrived(slot(owner), ring_recv.at[way, step], {"seq": right})

    pack(my_pair)
    pack(pair_at(1))
    send_x(sibling)
    xg_ref[:, me] = xs[me]
    last_right, last_left = n // 2, n // 2 - 1

    def lap(k, carry):
        @pl.when(k + 1 < pairs)
        def _():
            pack(pair_at(k + 1))

        p = pair_at(k)
        send_x(2 * p)
        send_x(2 * p + 1)
        from_left, from_right = lax.rem(me - k + n, n), lax.rem(me + k, n)
        take(from_left, k - 1, 0)
        ring(slot(from_left), from_left, k, 0)
        aside(slot(from_left), from_left)
        take(from_right, k - 1, 1)

        @pl.when(k < last_left)
        def _():
            ring(slot(from_right), from_right, k, 1)

        aside(slot(from_right), from_right)
        return carry

    lax.fori_loop(1, last_right, lap, 0)
    far = lax.rem(me + n - last_right, n)
    take(far, last_right - 1, 0)
    aside(slot(far), far)

    arrived(xg_ref.at[:, pl.ds(0, n - 1)], x_recv, {"seq": right})
    arrived(dtg_ref.at[pl.ds(0, n - 1)], dt_recv, {"seq": right})
    for k in range(1, quarters):
        from_g = lax.rem(g - k + quarters, quarters)
        arrived(
            bcg_ref.at[pl.ds(from_g * share, share)], side_recv.at[k - 1], {"seq": right}
        )
    sent(xg_ref.at[:, pl.ds(0, n - 1)], x_send, {"seq": right})
    sent(dtg_ref.at[pl.ds(0, n - 1)], dt_send, {"seq": right})
    for k in range(1, quarters):
        sent(bcg_ref.at[pl.ds(0, share)], side_send, {"seq": right})

    def drain(k, carry):
        sent(slot(me), ring_send.at[0, k], {"seq": right})

        @pl.when(k < last_left)
        def _():
            sent(slot(me), ring_send.at[1, k], {"seq": right})

        return carry

    lax.fori_loop(0, last_right, drain, 0)


def bring_in(x, bc, dt, n):
    pairs, _, sub, width = x.shape
    dma = pltpu.SemaphoreType.DMA
    return pl.pallas_call(
        in_kernel,
        out_shape=(
            jax.ShapeDtypeStruct((pairs, n, sub, LANES), bf16),
            jax.ShapeDtypeStruct(dt.shape, f32),
            jax.ShapeDtypeStruct((2 * pairs, n, sub, 2 * NSTATE), bf16),
        ),
        in_specs=[VM] * 3,
        out_specs=(VM,) * 3,
        scratch_shapes=[
            pltpu.VMEM((n, pairs, sub, LANES), bf16),
            dma, dma, dma, dma,
            dma((2, n // 2)), dma((2, n // 2)),
            dma, dma((4,)),
        ],
        compiler_params=pltpu.CompilerParams(
            collective_id=1, has_side_effects=True, vmem_limit_bytes=24 * 1024 * 1024
        ),
        cost_estimate=pl.CostEstimate(flops=1_000_000, bytes_accessed=200_000_000, transcendentals=0),
        name="bring_in",
    )(x, bc, dt)


def out_kernel(
    y_ref, ext_ref, gate_ref, gain_ref, w_hbm, out_ref, extg_ref,
    yg, feat, squares, sums, ms, mg, w_vmem, acc,
    y_send, y_recv, ext_send, ext_recv, f_send, f_recv, s_send, s_recv, m_send, m_recv, w_sem,
):
    pairs, n, sub, _ = y_ref.shape
    quarters = lax.axis_size("head")
    me, g = lax.axis_index("seq"), lax.axis_index("head")
    sibling = me + 1 - 2 * lax.rem(me, 2)
    my_pair = lax.div(me, 2)
    half = pairs * sub
    rows = 2 * half
    cols = out_ref.shape[1]
    inner = w_vmem.shape[0]
    right = {"seq": lax.rem(me + 1, n)}
    load_w = pltpu.make_async_copy(w_hbm, w_vmem, w_sem)
    load_w.start()
    greet()

    def send_y(to, k):
        copy_to(y_ref.at[:, to], yg.at[me], y_send, y_recv.at[k], {"seq": to}).start()

    def send_lap(k, carry):
        p = lax.rem(my_pair + offset_of(k) + pairs, pairs)
        send_y(2 * p, k)
        send_y(2 * p + 1, k)
        return carry

    send_y(sibling, 0)
    lax.fori_loop(1, pairs, send_lap, 0)

    def send_ext(k, carry):
        to = lax.rem(me + k, n)
        copy_to(ext_ref.at[to], extg_ref.at[me], ext_send, ext_recv, {"seq": to}).start()
        return carry

    lax.fori_loop(1, n, send_ext, 0)
    extg_ref[me] = ext_ref[me]
    yg[me] = y_ref[:, me]

    def unpack(p):
        lanes = pl.ds(pl.multiple_of(p * LANES, LANES), LANES)
        first = yg[2 * p].reshape(half, LANES).astype(f32)
        second = yg[2 * p + 1].reshape(half, LANES).astype(f32)
        for h, v in enumerate(swap_halves(first, second)):
            gate = gate_ref[:, h, :, lanes].reshape(half, LANES).astype(f32)
            gated = v * silu(gate)
            squares[h * half : (h + 1) * half, :] += gated * gated
            feat[g, p, h * half : (h + 1) * half, :] = (gated * gain_ref[:, lanes]).astype(bf16)

    def spread(p):
        for k in range(1, quarters):
            copy_to(
                feat.at[g, p], feat.at[g, p], f_send, f_recv.at[k - 1],
                {"head": lax.rem(g + k, quarters)},
            ).start()

    def from_pair(k):
        return lax.rem(my_pair - offset_of(k) + pairs, pairs)

    squares[...] = jnp.zeros(squares.shape, f32)
    arrived(yg.at[0], y_recv.at[0], right)
    unpack(my_pair)

    def lap(k, carry):
        arrived(yg.at[pl.ds(0, 2)], y_recv.at[k], right)
        unpack(from_pair(k))
        spread(from_pair(k - 1))
        return carry

    lax.fori_loop(1, pairs, lap, 0)
    total = jnp.broadcast_to(jnp.sum(squares[...], axis=1, keepdims=True), (rows, LANES))
    sums[g] = total.T[0:8, :]
    spread(from_pair(pairs - 1))
    for k in range(1, quarters):
        copy_to(
            sums.at[g], sums.at[g], s_send, s_recv.at[k - 1], {"head": lax.rem(g + k, quarters)}
        ).start()

    load_w.wait()
    acc[...] = jnp.zeros(acc.shape, f32)
    group = 4 if pairs % 4 == 0 else 1

    def project(owner):
        def step(t, carry):
            first = t * group
            lhs = jnp.concatenate([feat[owner, first + u] for u in range(group)], axis=1)
            at = owner * (pairs * LANES) + first * LANES
            rhs = w_vmem[pl.ds(pl.multiple_of(at, LANES), group * LANES), :]
            acc[...] += jnp.dot(lhs, rhs, preferred_element_type=f32)
            return carry

        lax.fori_loop(0, pairs // group, step, 0)

    project(g)
    for k in range(1, quarters):
        owner = lax.rem(g - k + quarters, quarters)
        arrived(feat.at[owner], f_recv.at[k - 1], right)
        arrived(sums.at[owner], s_recv.at[k - 1], right)
        project(owner)
    row_sum = sums[0]
    for k in range(1, quarters):
        row_sum = row_sum + sums[k]
    mean = jnp.broadcast_to(row_sum[0:1, :], (LANES, rows)).T * (1.0 / inner)
    scale = lax.rsqrt(mean + EPS)
    for q in range(cols // LANES):
        part = slice(q * LANES, (q + 1) * LANES)
        for h in range(2):
            here = slice(h * half, (h + 1) * half)
            block = (acc[here, part] * scale[here, :]).astype(bf16)
            ms[:, h, :, part] = block.reshape(pairs, sub, LANES)

    def send_m(k, carry):
        to = lax.rem(me + offset_of(k) + n, n)
        copy_to(
            ms.at[lax.div(to, 2), lax.rem(to, 2)], mg.at[me], m_send, m_recv, {"seq": to}
        ).start()
        return carry

    mg[me] = ms[my_pair, lax.rem(me, 2)]
    lax.fori_loop(1, n, send_m, 0)

    sent(yg.at[pl.ds(0, n - 1)], y_send, right)
    sent(extg_ref.at[pl.ds(0, n - 1)], ext_send, right)
    for k in range(1, quarters):
        sent(feat.at[0], f_send, right)
        sent(sums.at[0], s_send, right)
    arrived(extg_ref.at[pl.ds(0, n - 1)], ext_recv, right)
    arrived(mg.at[pl.ds(0, n - 1)], m_recv, right)
    for q in range(cols // LANES):
        part = slice(q * LANES, (q + 1) * LANES)
        out_ref[:, part] = mg[:, :, part].reshape(n * sub, LANES)
    sent(mg.at[pl.ds(0, n - 1)], m_send, right)


def take_out(y, ext, gate, gain, weight):
    pairs, n, sub, _ = y.shape
    inner, cols = weight.shape
    rows = 2 * pairs * sub
    quarters = inner // gain.shape[1]
    dma = pltpu.SemaphoreType.DMA
    return pl.pallas_call(
        out_kernel,
        out_shape=(
            jax.ShapeDtypeStruct((n * sub, cols), bf16),
            jax.ShapeDtypeStruct(ext.shape, bf16),
        ),
        in_specs=[VM] * 4 + [ANY],
        out_specs=(VM, VM),
        scratch_shapes=[
            pltpu.VMEM((n, pairs, sub, LANES), bf16),
            pltpu.VMEM((quarters, pairs, rows, LANES), bf16),
            pltpu.VMEM((rows, LANES), f32),
            pltpu.VMEM((quarters, 8, rows), f32),
            pltpu.VMEM((pairs, 2, sub, cols), bf16),
            pltpu.VMEM((n, sub, cols), bf16),
            pltpu.VMEM((inner, cols), bf16),
            pltpu.VMEM((rows, cols), f32),
            dma, dma((pairs,)), dma, dma, dma, dma((4,)), dma, dma((4,)), dma, dma, dma,
        ],
        compiler_params=pltpu.CompilerParams(
            collective_id=2, has_side_effects=True, vmem_limit_bytes=32 * 1024 * 1024
        ),
        cost_estimate=pl.CostEstimate(flops=1_000_000_000, bytes_accessed=200_000_000, transcendentals=0),
        name="take_out",
    )(y, ext, gate, gain, weight)


def head_kernel(
    start_ref, par_ref, wbc_ref, x_ref, dt_ref, bc_ref,
    y_ref, hi_ref, lo_ref,
    cum_ref, w_ref, step_ref, extx_ref, extbc_ref, bc_conv_ref, s_ref,
):
    pairs, n, sub, _ = x_ref.shape
    span = n * sub
    blocks = 2 * pairs
    start = start_ref[0]
    row = lax.broadcasted_iota(jnp.int32, (span, LANES), 0)
    lane = lax.broadcasted_iota(jnp.int32, (span, LANES), 1)
    odd = lane >= HEAD_DIM

    pos = lax.broadcasted_iota(jnp.int32, (blocks, span), 0) * span + lax.broadcasted_iota(
        jnp.int32, (blocks, span), 1
    )
    live = (pos >= start).astype(f32)
    step = softplus(dt_ref[...].astype(f32) + par_ref[5:6, :]) * live
    log_decay = -par_ref[4:5, :] * step
    upto = (row <= lane).astype(f32)
    cum = jnp.dot(log_decay, upto, precision=highest, preferred_element_type=f32)
    cum_ref[...] = cum
    w_ref[...] = jnp.exp(cum[:, span - 1 : span] - cum) * step
    step_ref[...] = step

    extx_ref[0:8, :] = jnp.zeros((8, LANES), f32)
    extbc_ref[0:8, :] = jnp.zeros((8, 2 * NSTATE), f32)
    s_ref[...] = jnp.zeros(s_ref.shape, f32)
    causal = row >= lane
    low8 = lax.broadcasted_iota(jnp.int32, (8, LANES), 1) >= HEAD_DIM

    def pair(i, carry):
        base = i * (2 * span)
        live_x = (base + jnp.where(odd, span, 0) + row) >= start
        xf = jnp.where(live_x, x_ref[i].reshape(span, LANES).astype(f32), 0.0)
        last = pltpu.roll(xf[span - 8 :, :], HEAD_DIM, 1)
        extx_ref[0:8, :] = jnp.where(low8, last, extx_ref[0:8, :])
        extx_ref[8 : 8 + span, :] = xf
        acc = jnp.zeros((span, LANES), f32)
        for k in range(KCONV):
            acc = acc + par_ref[k : k + 1, :] * extx_ref[pl.ds(8 - (KCONV - 1) + k, span), :]
        extx_ref[0:8, :] = last
        xc = silu(acc).astype(bf16)
        xcf = xc.astype(f32)

        rows1 = lax.broadcasted_iota(jnp.int32, (span, 2 * NSTATE), 0)
        for h in range(2):
            raw = bc_ref[2 * i + h].reshape(span, 2 * NSTATE).astype(f32)
            bcf = jnp.where(base + h * span + rows1 >= start, raw, 0.0)
            extbc_ref[8 + h * span : 8 + (h + 1) * span, :] = bcf
        acc2 = jnp.zeros((2 * span, 2 * NSTATE), f32)
        for k in range(KCONV):
            acc2 = acc2 + wbc_ref[k : k + 1, :] * extbc_ref[pl.ds(8 - (KCONV - 1) + k, 2 * span), :]
        extbc_ref[0:8, :] = bcf[span - 8 :, :]
        bc_conv_ref[...] = silu(acc2).astype(bf16)

        state = s_ref[...]
        ys, ecs, wcs, decays, bs, cs = [], [], [], [], [], []
        for h in range(2):
            c = 2 * i + h
            b_blk = bc_conv_ref[h * span : (h + 1) * span, 0:NSTATE]
            c_blk = bc_conv_ref[h * span : (h + 1) * span, NSTATE : 2 * NSTATE]
            cum_row = cum_ref[pl.ds(c, 1), :]
            cum_b = jnp.broadcast_to(cum_row, (span, span))
            cum_c = cum_b.T
            w_c = jnp.broadcast_to(w_ref[pl.ds(c, 1), :], (span, span)).T
            seg = jnp.exp(jnp.where(causal, cum_c - cum_b, -1e30))
            scores = lax.dot_general(
                c_blk, b_blk, (((1,), (1,)), ((), ())), preferred_element_type=f32
            )
            mix = (scores * seg * step_ref[pl.ds(c, 1), :]).astype(bf16)
            ys.append(jnp.dot(mix, xc, preferred_element_type=f32))
            e_c = jnp.exp(cum_c)
            ecs.append(e_c)
            wcs.append(w_c)
            decays.append(e_c[span - 1 : span, :])
            bs.append(b_blk)
            cs.append(c_blk)
        scaled = (jnp.where(odd, wcs[1], wcs[0]) * xcf).astype(bf16)
        adds = [
            lax.dot_general(b, scaled, (((0,), (0,)), ((), ())), preferred_element_type=f32)
            for b in bs
        ]
        after_even = decays[0] * state + adds[0]
        entering = jnp.where(odd, pltpu.roll(after_even, HEAD_DIM, 1), state)
        ent_hi = entering.astype(bf16)
        ent_lo = (entering - ent_hi.astype(f32)).astype(bf16)
        outs = []
        for h in range(2):
            from_state = jnp.dot(cs[h], ent_hi, preferred_element_type=f32) + jnp.dot(
                cs[h], ent_lo, preferred_element_type=f32
            )
            outs.append(ys[h] + ecs[h] * from_state)
        y = jnp.where(odd, outs[1], outs[0]) + par_ref[6:7, :] * xcf
        y_ref[i] = y.astype(bf16).reshape(n, sub, LANES)
        after_odd = decays[1] * entering + adds[1]
        s_ref[...] = pltpu.roll(after_odd, HEAD_DIM, 1)
        return carry

    lax.fori_loop(0, pairs, pair, 0)
    final = s_ref[...].T[0:HEAD_DIM, :]
    hi = final.astype(bf16)
    hi_ref[...] = hi
    lo_ref[...] = (final - hi.astype(f32)).astype(bf16)


def run_head(start, par, wbc, x, dt, bc):
    pairs, n, sub, _ = x.shape
    span = n * sub
    vmem = pl.BlockSpec(memory_space=pltpu.VMEM)
    return pl.pallas_call(
        head_kernel,
        out_shape=(
            jax.ShapeDtypeStruct(x.shape, bf16),
            jax.ShapeDtypeStruct((HEAD_DIM, NSTATE), bf16),
            jax.ShapeDtypeStruct((HEAD_DIM, NSTATE), bf16),
        ),
        in_specs=[pl.BlockSpec(memory_space=pltpu.SMEM)] + [vmem] * 5,
        out_specs=(vmem, vmem, vmem),
        scratch_shapes=[
            pltpu.VMEM((2 * pairs, span), f32),
            pltpu.VMEM((2 * pairs, span), f32),
            pltpu.VMEM((2 * pairs, span), f32),
            pltpu.VMEM((8 + span, LANES), f32),
            pltpu.VMEM((8 + 2 * span, 2 * NSTATE), f32),
            pltpu.VMEM((2 * span, 2 * NSTATE), bf16),
            pltpu.VMEM((NSTATE, LANES), f32),
        ],
        compiler_params=pltpu.CompilerParams(vmem_limit_bytes=32 * 1024 * 1024),
        cost_estimate=pl.CostEstimate(flops=1_000_000_000, bytes_accessed=5_000_000, transcendentals=3_000_000),
        name="head_scan",
    )(start, par, wbc, x, dt, bc)


def local(
    x_proj, gate_proj, bc_proj, dt_proj, a_rate, dt_bias, d_skip,
    conv_x_weight, conv_bc_weight, norm_gain, out_weight, request_first_position, owner,
):
    _, blocks, _, sub, width = x_proj.shape
    n = lax.axis_size("seq")
    me = lax.axis_index("seq")
    pairs = blocks // 2
    span = n * sub
    start = request_first_position
    weight = lax.all_gather(out_weight, ("seq", "rep"), axis=0, tiled=True)

    dt_send = dt_proj.reshape(blocks * sub, n).T.reshape(n, 1, blocks * sub).astype(f32)
    x_head, dt_got, bc_all = bring_in(
        x_proj.reshape(pairs, 2, sub, width), bc_proj.reshape(blocks, sub, 2 * NSTATE), dt_send, n
    )
    dt_head = dt_got.reshape(n, blocks, sub).transpose(1, 0, 2).reshape(blocks, span)

    heads = jnp.stack([a_rate, dt_bias, d_skip, jnp.zeros_like(a_rate)])
    taps = conv_x_weight.reshape(KCONV, n, HEAD_DIM)
    par_all = jnp.concatenate(
        [
            jnp.concatenate([taps, taps], axis=2),
            jnp.broadcast_to(heads[:, :, None], heads.shape + (LANES,)),
        ],
        axis=0,
    )
    par = lax.dynamic_index_in_dim(par_all, me, 1, keepdims=False)
    y, hi, lo = run_head(start, par, conv_bc_weight, x_head, dt_head, bc_all)

    places = jnp.arange(n, dtype=jnp.int32)
    slab_of = jnp.sum(jnp.where(owner[0][None, :] == places[:, None], places[None, :], 0), axis=1)
    my_slab = slab_of[me]
    per = HEAD_DIM // n * NSTATE // LANES
    keep = KCONV - 1
    used = 2 * per + keep
    spare = -used % 8
    live_tail = blocks * span - keep + jnp.arange(keep, dtype=jnp.int32) >= start[0]
    tail_x = jnp.where(live_tail[:, None], x_head[pairs - 1, n - 1, sub - keep :], jnp.zeros((), bf16))
    slabs = jnp.take(
        jnp.concatenate([hi.reshape(n, per, LANES), lo.reshape(n, per, LANES)], axis=1), slab_of, axis=0
    )
    ext = jnp.concatenate(
        [
            slabs,
            jnp.broadcast_to(tail_x[None], (n, keep, LANES)),
            jnp.zeros((n, spare, LANES), bf16),
        ],
        axis=1,
    )
    mixed, ext_got = take_out(
        y, ext, gate_proj.reshape(pairs, 2, sub, width), norm_gain[None], weight
    )
    state = ext_got[:, :per].astype(f32) + ext_got[:, per : 2 * per].astype(f32)
    conv_x_state = lax.dynamic_index_in_dim(
        ext_got[:, 2 * per : used, HEAD_DIM:], my_slab, 0
    )[None]
    tail_bc = jnp.where(live_tail[:, None], bc_all[blocks - 1, n - 1, sub - keep :], jnp.zeros((), bf16))
    conv_bc_state = lax.dynamic_index_in_dim(
        tail_bc.reshape(keep, n, -1), my_slab, axis=1, keepdims=False
    )[None, None]
    return (mixed[None], state.reshape(1, 1, n, per * LANES), conv_x_state, conv_bc_state)


def solution(mesh):
    return jax.shard_map(
        local,
        mesh=mesh,
        in_specs=(
            P(("grp", "rep"), None, "seq", None, "head"),
            P(("grp", "rep"), None, "seq", None, "head"),
            P(("grp", "rep"), None, "seq", None, None),
            P(("grp", "rep"), None, "seq", None, "head"),
            P("head"),
            P("head"),
            P("head"),
            P(None, "head"),
            P(),
            P("head"),
            P(("seq", "rep"), "head"),
            P(("grp", "rep")),
            P(("grp", "rep"), None),
        ),
        out_specs=(
            P(("grp", "rep"), "seq", "head"),
            P(("grp", "rep"), "seq", "head", None),
            P(("grp", "rep"), "seq", None, "head"),
            P(("grp", "rep"), "seq", None, None),
        ),
        check_vma=False,
    )
```

time: 555 us -> 318 us (0.57)
  waiting for transfers between devices: 389 us -> 42.5 us
  Pallas kernels: 13 us -> 241 us
  starting transfers between devices: 71.7 us -> 0.06 us
  local copies, waits for them, and re-layouts: 35.9 us -> 13.8 us
  blocking collectives: 11.5 us -> 0 us
  other arithmetic: 9.79 us -> 2.03 us
    pallas_call x1 -> x3, Pallas kernels: 13 us -> 241 us  [the longest x1 134 us: bring_in(): pl.pallas_call(in_kernel, out_shape=(jax.ShapeDtypeStruct((pairs, n, sub,...]
    all_gather x2 -> x0, waiting for transfers between devices: 172 us -> none  [the longest x1 146 us: local(): bc_all = lax.all_gather(bc_proj.reshape(blocks, sub, 2 * NSTATE), 'seq')]
    all_gather x1, waiting for transfers between devices: 144 us -> 41.8 us  [local(): weight = lax.all_gather(out_weight, ('seq', 'rep'), axis=0, tiled=True)]
    all_to_all x3 -> x0, waiting for transfers between devices: 72.4 us -> none  [exchange(): return lax.all_to_all(value, axis, split_axis=0, concat_axis=0, tiled=True)]
    all_to_all x3 -> x0, starting transfers between devices: 71.3 us -> none  [exchange(): return lax.all_to_all(value, axis, split_axis=0, concat_axis=0, tiled=True)]
    psum x1 -> x0, blocking collectives: 11.5 us -> none  [local(): squares = lax.psum(jnp.sum(gated * gated, axis=1), 'head')]
    convert_element_type x5 -> x1, local copies, waits for them, and re-layouts: 11.9 us -> 0.81 us  [local(): dt_proj.reshape(blocks * sub, n).T.reshape(n, 1, blocks * sub).astype(f32)]
    unnamed x26 -> x14, local copies, waits for them, and re-layouts: 1.34 us -> 8.93 us
  transfers between devices with their start and end apart: 6 -> 1, of which waited for: 5 -> 1; matrix products, arithmetic and copies ran while one was open for 3% -> 2% of each run, Pallas kernels for 0% -> 47%
where the time goes in v2:
time: 318 us; the launch traced here: 317 us
  Pallas kernels  241 us (76%)
  waiting for transfers between devices  42.5 us (13%)
  between operations  16.8 us (5%)
  local copies, waits for them, and re-layouts  13.8 us (4%)
    pallas_call x1, Pallas kernels, bring_in(): pl.pallas_call(in_kernel, out_shape=(jax.ShapeDtypeStruct((pairs, n, sub,...  134 us
    pallas_call x1, Pallas kernels, take_out(): pl.pallas_call(out_kernel, out_shape=(jax.ShapeDtypeStruct((n * sub, cols...  93.8 us
    all_gather x1, waiting for transfers between devices, local(): weight = lax.all_gather(out_weight, ('seq', 'rep'), axis=0, tiled=True)  41.8 us
    pallas_call x1, Pallas kernels, run_head(): pl.pallas_call(head_kernel, out_shape=(jax.ShapeDtypeStruct(x.shape, bf16...  13.3 us
    unnamed x14, local copies, waits for them, and re-layouts  8.93 us
  transfers between devices with their start and end apart: 1, of which 1 were waited for; matrix products, arithmetic and copies ran while one was open for 2% of the time, Pallas kernels for 47%

profile of v2, /device:TPU:40, one launch (start us, length us, event | category | flops | bytes accessed | tf_op | source)
XLA Modules:
  0.0 316.6 jit_solution(15019297789227494162)
XLA Ops:
  7.2 0.7 all-gather.2.cloned.1.call-update
  8.0 0.8 select_reduce_fusion
  8.7 0.6 dynamic_slice.16
  10.6 0.9 reshape.90
  11.5 0.1 pad.11.clone
  11.6 0.8 maximum_maximum_fusion.1
  12.4 0.1 copy.39
  12.5 0.8 copy.40
  13.3 1.1 copy-done.1
  14.3 0.8 copy-done.3
  15.2 134.3 %bring_in.1 = (bf16[16,32,4,128]{3,2,1,0:T(4,128)(2,1)S(1)}, f32[32,1,128]{2,1,0:T(1,128)S(1)}, bf16[32,32,4,256]{3,2,1,0:T(4,128)(2,1)S(1)}) custom-call(bf16[16,2,4,2048]{3,2,1,0:T(4,128)(2,1)S(1)} %bitcast.38, bf16[32,4,256]{2,1,0:T(4,128)(2,1)S(1)} %bitcast.41, f32[32,1,128]{2,1,0:T(1,128)S(1)} %bitcast.42), custom_call_target="tpu_custom_call" | custom-call | flops 1000000 | bytes 200000000 | tf_op jit(solution)/shard_map/bring_in/pallas_call | solution.py:196
  149.5 0.1 copy.41
  149.6 0.1 copy.42
  150.4 0.1 squeeze.22
  151.2 0.1 broadcast_select_fusion.1
  151.3 0.6 copy.46
  151.9 0.1 broadcast_in_dim.77
  152.0 0.1 fusion.2.par_ref
  152.0 0.7 copy-done.5
  152.7 13.3 %head_scan.1 = (bf16[16,32,4,128]{3,2,1,0:T(4,128)(2,1)S(1)}, bf16[64,128]{1,0:T(8,128)(2,1)S(1)}, bf16[64,128]{1,0:T(8,128)(2,1)S(1)}) custom-call(s32[1]{0:T(128)} %copy.48.start_ref, f32[8,128]{1,0:T(8,128)S(1)} %fusion.2.par_ref, f32[4,256]{1,0:T(4,128)S(1)} %copy-done.5, bf16[16,32,4,128]{3,2,1,0:T(4,128)(2,1)S(1)} %get-tuple-element.12.x_ref, ...), custom_call_target="tpu_custom_call" | custom-call | flops 1000000000 | bytes 5000000 | tf_op jit(solution)/shard_map/head_scan/pallas_call | solution.py:497
  166.1 0.6 gather_fusion
  166.9 0.1 broadcast_select_fusion
  167.0 0.1 maximum_maximum_fusion.ext_ref
  167.1 41.8 %all-gather.2.cloned.1.call-done.w_hbm = bf16[8192,512]{1,0:T(8,128)(2,1)} async-done(((bf16[128,512]{1,0:T(8,128)(2,1)}), bf16[8192,512]{1,0:T(8,128)(2,1)}) %all-gather.2.cloned.1.call-update) | async-done | bytes 8388624 | tf_op jit(solution)/shard_map/all_gather | solution.py:531
  208.9 3.4 %copy-done = bf16[8192,512]{1,0:T(8,128)(2,1)S(1)} copy-done((bf16[8192,512]{1,0:T(8,128)(2,1)S(1)}, bf16[8192,512]{1,0:T(8,128)(2,1)}, u32[]{:S(2)}) %copy-start) | copy-done | bytes 8388632
  212.2 1.0 copy-done.2
  213.3 0.7 copy-done.4
  214.0 93.8 %take_out.1 = (bf16[128,512]{1,0:T(8,128)(2,1)S(1)}, bf16[32,8,128]{2,1,0:T(8,128)(2,1)S(1)}) custom-call(bf16[16,32,4,128]{3,2,1,0:T(4,128)(2,1)S(1)} %get-tuple-element.15.y_ref, bf16[32,8,128]{2,1,0:T(8,128)(2,1)S(1)} %maximum_maximum_fusion.ext_ref, bf16[16,2,4,2048]{3,2,1,0:T(4,128)(2,1)S(1)} %bitcast.39, f32[1,2048]{1,0:T(1,128)S(1)} %bitcast.45, ...), custom_call_target="tpu_custom_call" | custom-call | flops 1000000000 | bytes 200000000 | tf_op jit(solution)/shard_map/take_out/pallas_call | solution.py:360
  307.8 0.1 slice.18
  307.9 0.6 fusion.3
  308.5 0.6 reshape.98
  309.1 0.7 copy.49
  (19 shorter events, 0.4 us)
Async XLA Ops:
  7.2 201.7 %all-gather.2.cloned.1.call-start = ((), (), s32[]{:S(2)}) async-start(), calls=%async_computation | async-start | bytes 8519680 | tf_op jit(solution)/shard_map/all_gather | solution.py:531
  13.3 1.1 copy-start.1
  14.3 0.8 copy-start.3
  152.0 0.7 copy-start.5
  208.9 3.4 %copy-start = (bf16[8192,512]{1,0:T(8,128)(2,1)S(1)}, bf16[8192,512]{1,0:T(8,128)(2,1)}, u32[]{:S(2)}) copy-start(bf16[8192,512]{1,0:T(8,128)(2,1)} %all-gather.2.cloned.1.call-done.w_hbm) | copy-start | bytes 25165828
  212.2 1.0 copy-start.2
  213.3 0.7 copy-start.4
Sparse Core Ops, SparseCore 0:
  10.1 198.6 all-gather.1

commit v3 on v1

v3 whole, which is shorter than its diff:
```python
import functools

import jax
import jax.numpy as jnp
from jax import lax
from jax.experimental import pallas as pl
from jax.experimental.pallas import tpu as pltpu
from jax.sharding import PartitionSpec as P

HEAD_DIM = 64
NSTATE = 128
KCONV = 4
EPS = 1e-05
LANES = 128
MESH = pl.DeviceIdType.MESH
VM = pl.BlockSpec(memory_space=pltpu.VMEM)
SM = pl.BlockSpec(memory_space=pltpu.SMEM)

highest = lax.Precision.HIGHEST
f32, bf16 = jnp.float32, jnp.bfloat16


def silu(v):
    return v * (1.0 / (1.0 + jnp.exp(-v)))


def softplus(v):
    return jnp.maximum(v, 0.0) + jnp.log1p(jnp.exp(-jnp.abs(v)))


def copy_to(src, dst, send_sem, recv_sem, device):
    return pltpu.make_async_remote_copy(
        src_ref=src, dst_ref=dst, send_sem=send_sem, recv_sem=recv_sem,
        device_id=device, device_id_type=MESH,
    )


def arrived(region, sem, device):
    copy_to(region, region, sem, sem, device).wait_recv()


def sent(region, sem, device):
    copy_to(region, region, sem, sem, device).wait_send()


def greet(axes):
    barrier = pltpu.get_barrier_semaphore()
    total = 0
    for axis in axes:
        size, here = lax.axis_size(axis), lax.axis_index(axis)

        def hello(k, carry):
            pl.semaphore_signal(
                barrier, inc=1, device_id={axis: lax.rem(here + k, size)}, device_id_type=MESH
            )
            return carry

        lax.fori_loop(1, size, hello, 0)
        total += size - 1
    pl.semaphore_wait(barrier, total)


def offset_of(k):
    half = lax.div(k + 1, 2)
    return jnp.where(lax.rem(k, 2) == 1, half, -half)


def swap_halves(a, b):
    low = lax.broadcasted_iota(jnp.int32, a.shape, 1) < HEAD_DIM
    return (
        jnp.where(low, a, pltpu.roll(b, HEAD_DIM, 1)),
        jnp.where(low, pltpu.roll(a, HEAD_DIM, 1), b),
    )


def layer_kernel(
    start_ref, a_ref, bias_ref, skip_ref, owner_ref, taps_ref, wbc_ref, gain_ref,
    dt_ref, bc_ref, x_ref, w_ref, gate_ref,
    out_ref, state_out, tailx_out, tailbc_out,
    xs, xg, dts, dtg, bcg, wall, yl, yg, feat, squares, sums, ms, mg, acc, slabs, tails, fin, wide,
    cum_ref, wgt_ref, step_ref, extx_ref, extbc_ref, bc_conv_ref, s_ref,
    x_send, x_recv, dt_send, dt_recv, ring_send, ring_recv, side_send, side_recv,
    wring_send, wring_recv, wsib_send, wsib_recv, wgrp_send, wgrp_recv,
    tail_send, tail_recv, y_send, y_recv, st_send, st_recv, f_send, f_recv, q_send, q_recv,
    m_send, m_recv,
):
    pairs, _, sub, _ = x_ref.shape
    blocks = 2 * pairs
    n, quarters = lax.axis_size("seq"), lax.axis_size("head")
    reps, groups = lax.axis_size("rep"), lax.axis_size("grp")
    me, g = lax.axis_index("seq"), lax.axis_index("head")
    rep, grp = lax.axis_index("rep"), lax.axis_index("grp")
    span = n * sub
    half = pairs * sub
    rows = 2 * half
    cols = out_ref.shape[1]
    inner = wall.shape[0]
    share = blocks // quarters
    last_right, last_left = n // 2, n // 2 - 1
    right, left = lax.rem(me + 1, n), lax.rem(me + n - 1, n)
    to_right = {"seq": right}
    sibling = me + 1 - 2 * lax.rem(me, 2)
    my_pair = lax.div(me, 2)
    mine = bc_ref.at[pl.ds(g * share, share)]
    piece = w_ref.shape[0]
    part_rows = piece // groups
    start = start_ref[0]

    greet(("seq", "head", "rep", "grp"))

    def slot(owner):
        return bcg.at[pl.ds(g * share, share), owner]

    def wslot(owner, which):
        at = (owner * reps + rep) * piece + which * part_rows
        return wall.at[pl.ds(pl.multiple_of(at, 16), part_rows)]

    def ring(src, wsrc, owner, step, way):
        there = {"seq": right if way == 0 else left}
        copy_to(src, slot(owner), ring_send.at[way, step], ring_recv.at[way, step], there).start()
        copy_to(
            wsrc, wslot(owner, grp), wring_send.at[way, step], wring_recv.at[way, step], there
        ).start()

    def aside(src, owner):
        for k in range(1, quarters):
            copy_to(
                src, slot(owner), side_send, side_recv.at[k - 1],
                {"head": lax.rem(g + k, quarters)},
            ).start()

    def to_sibling(src, dst):
        if reps == 2:
            copy_to(src, dst, wsib_send, wsib_recv, {"rep": 1 - rep}).start()

    def hand_on(owner):
        block = wslot(owner, grp)
        to_sibling(block, block)
        for k in range(1, groups):
            copy_to(
                block, block, wgrp_send, wgrp_recv.at[k - 1], {"grp": lax.rem(grp + k, groups)}
            ).start()

    own_rows = pl.ds(pl.multiple_of((me * reps + rep) * piece, 16), piece)
    own_part = w_ref.at[pl.ds(pl.multiple_of(grp * part_rows, 16), part_rows)]
    ring(mine, own_part, me, 0, 0)
    ring(mine, own_part, me, 0, 1)
    aside(mine, me)
    to_sibling(w_ref, wall.at[own_rows])
    bcg[pl.ds(g * share, share), me] = bc_ref[pl.ds(g * share, share)]
    wall[own_rows, :] = w_ref[...]

    def pack(p):
        lanes = pl.ds(pl.multiple_of(p * LANES, LANES), LANES)
        even = x_ref[:, 0, :, lanes].reshape(half, LANES).astype(f32)
        odd = x_ref[:, 1, :, lanes].reshape(half, LANES).astype(f32)
        first, second = swap_halves(even, odd)
        xs[2 * p] = first.astype(bf16).reshape(pairs, sub, LANES)
        xs[2 * p + 1] = second.astype(bf16).reshape(pairs, sub, LANES)

    def send_x(to):
        copy_to(xs.at[to], xg.at[:, me], x_send, x_recv, {"seq": to}).start()

    def pair_at(k):
        return lax.rem(my_pair + offset_of(k) + pairs, pairs)

    pack(my_pair)
    pack(pair_at(1))
    send_x(sibling)
    xg[:, me] = xs[me]
    dt_t = dt_ref[...].astype(f32).reshape(blocks * sub, n).T
    dts[...] = dt_t.reshape(n, 1, blocks * sub)

    def lap(k, carry):
        @pl.when(k + 1 < pairs)
        def _():
            pack(pair_at(k + 1))

        @pl.when(k < pairs)
        def _():
            p = pair_at(k)
            send_x(2 * p)
            send_x(2 * p + 1)

        from_left, from_right = lax.rem(me - k + n, n), lax.rem(me + k, n)
        arrived(slot(from_left), ring_recv.at[0, k - 1], to_right)
        arrived(wslot(from_left, grp), wring_recv.at[0, k - 1], to_right)
        ring(slot(from_left), wslot(from_left, grp), from_left, k, 0)
        aside(slot(from_left), from_left)
        hand_on(from_left)
        arrived(slot(from_right), ring_recv.at[1, k - 1], to_right)
        arrived(wslot(from_right, grp), wring_recv.at[1, k - 1], to_right)

        @pl.when(k < last_left)
        def _():
            ring(slot(from_right), wslot(from_right, grp), from_right, k, 1)

        aside(slot(from_right), from_right)
        hand_on(from_right)
        return carry

    def dt_out(k, carry):
        to = lax.rem(me + offset_of(k) + n, n)
        copy_to(dts.at[to], dtg.at[me], dt_send, dt_recv, {"seq": to}).start()
        return carry

    lax.fori_loop(1, n, dt_out, 0)
    dtg[me] = dts[me]
    lax.fori_loop(1, last_right, lap, 0)
    far = lax.rem(me + n - last_right, n)
    arrived(slot(far), ring_recv.at[0, last_right - 1], to_right)
    arrived(wslot(far, grp), wring_recv.at[0, last_right - 1], to_right)
    aside(slot(far), far)
    hand_on(far)

    eye = lax.broadcasted_iota(jnp.int32, (n, n), 0) == owner_ref[...]
    chosen = eye.astype(bf16)
    wide[...] = xs[:, pairs - 1].astype(f32).reshape(n * sub, LANES)
    for r in range(sub - KCONV + 1, sub):
        picked = jnp.dot(
            chosen, wide[pl.ds(r, n, stride=sub), :].astype(bf16), preferred_element_type=f32
        )
        live_tail = (blocks - 1) * span + (n - 1) * sub + r >= start
        wide[pl.ds(r, n, stride=sub), :] = jnp.where(live_tail, picked, 0.0)
    tails[...] = wide[...].astype(bf16).reshape(n, sub, LANES)

    arrived(xg.at[:, pl.ds(0, n - 1)], x_recv, to_right)
    arrived(dtg.at[pl.ds(0, n - 1)], dt_recv, to_right)
    for k in range(1, quarters):
        from_g = lax.rem(g - k + quarters, quarters)
        arrived(bcg.at[pl.ds(from_g * share, share)], side_recv.at[k - 1], to_right)

    @pl.when(me == n - 1)
    def _():
        def send_tail(k, carry):
            to = lax.rem(me + k, n)
            copy_to(tails.at[to], tailx_out, tail_send, tail_recv, {"seq": to}).start()
            return carry

        lax.fori_loop(1, n, send_tail, 0)
        tailx_out[...] = tails[n - 1]

    tailbc_out[...] = bcg[blocks - 1, n - 1]

    row = lax.broadcasted_iota(jnp.int32, (span, LANES), 0)
    lane = lax.broadcasted_iota(jnp.int32, (span, LANES), 1)
    odd = lane >= HEAD_DIM
    own_lanes = pl.ds(pl.multiple_of(my_pair * LANES, LANES), LANES)
    tap_pair = taps_ref[:, own_lanes]
    tap_low = lax.broadcasted_iota(jnp.int32, (KCONV, LANES), 1) < HEAD_DIM
    taps = jnp.where(
        tap_low == (lax.rem(me, 2) == 0), tap_pair, pltpu.roll(tap_pair, HEAD_DIM, 1)
    )
    skip = skip_ref[me]

    by_piece = dtg[...].reshape(n, blocks * sub)
    dt = jnp.zeros((blocks, span), f32)
    for r in range(sub):
        pick = (
            lax.broadcasted_iota(jnp.int32, (blocks * sub, blocks), 0)
            == lax.broadcasted_iota(jnp.int32, (blocks * sub, blocks), 1) * sub + r
        ).astype(bf16)
        put = (
            lax.broadcasted_iota(jnp.int32, (n, span), 1)
            == lax.broadcasted_iota(jnp.int32, (n, span), 0) * sub + r
        ).astype(bf16)
        one = jnp.dot(by_piece.astype(bf16), pick, preferred_element_type=f32).astype(bf16)
        dt = dt + lax.dot_general(one, put, (((0,), (0,)), ((), ())), preferred_element_type=f32)
    pos = lax.broadcasted_iota(jnp.int32, (blocks, span), 0) * span + lax.broadcasted_iota(
        jnp.int32, (blocks, span), 1
    )
    step = softplus(dt + bias_ref[me]) * (pos >= start).astype(f32)
    log_decay = -a_ref[me] * step
    upto = (row <= lane).astype(f32)
    cum = jnp.dot(log_decay, upto, precision=highest, preferred_element_type=f32)
    cum_ref[...] = cum
    wgt_ref[...] = jnp.exp(cum[:, span - 1 : span] - cum) * step
    step_ref[...] = step

    extx_ref[0:8, :] = jnp.zeros((8, LANES), f32)
    extbc_ref[0:8, :] = jnp.zeros((8, 2 * NSTATE), f32)
    s_ref[...] = jnp.zeros(s_ref.shape, f32)
    causal = row >= lane
    odd8 = lax.broadcasted_iota(jnp.int32, (8, LANES), 1) >= HEAD_DIM

    def pair(i, carry):
        base = i * (2 * span)
        live_x = (base + jnp.where(odd, span, 0) + row) >= start
        xf = jnp.where(live_x, xg[i].reshape(span, LANES).astype(f32), 0.0)
        last = pltpu.roll(xf[span - 8 :, :], HEAD_DIM, 1)
        extx_ref[0:8, :] = jnp.where(odd8, last, extx_ref[0:8, :])
        extx_ref[8 : 8 + span, :] = xf
        acc = jnp.zeros((span, LANES), f32)
        for k in range(KCONV):
            acc = acc + taps[k : k + 1, :] * extx_ref[pl.ds(8 - (KCONV - 1) + k, span), :]
        extx_ref[0:8, :] = last
        xc = silu(acc).astype(bf16)
        xcf = xc.astype(f32)

        rows1 = lax.broadcasted_iota(jnp.int32, (span, 2 * NSTATE), 0)
        for h in range(2):
            raw = bcg[2 * i + h].reshape(span, 2 * NSTATE).astype(f32)
            bcf = jnp.where(base + h * span + rows1 >= start, raw, 0.0)
            extbc_ref[8 + h * span : 8 + (h + 1) * span, :] = bcf
        acc2 = jnp.zeros((2 * span, 2 * NSTATE), f32)
        for k in range(KCONV):
            acc2 = acc2 + wbc_ref[k : k + 1, :] * extbc_ref[pl.ds(8 - (KCONV - 1) + k, 2 * span), :]
        extbc_ref[0:8, :] = bcf[span - 8 :, :]
        bc_conv_ref[...] = silu(acc2).astype(bf16)

        state = s_ref[...]
        ys, ecs, wcs, decays, bs, cs = [], [], [], [], [], []
        for h in range(2):
            c = 2 * i + h
            b_blk = bc_conv_ref[h * span : (h + 1) * span, 0:NSTATE]
            c_blk = bc_conv_ref[h * span : (h + 1) * span, NSTATE : 2 * NSTATE]
            cum_row = cum_ref[pl.ds(c, 1), :]
            cum_b = jnp.broadcast_to(cum_row, (span, span))
            cum_c = cum_b.T
            w_c = jnp.broadcast_to(wgt_ref[pl.ds(c, 1), :], (span, span)).T
            seg = jnp.exp(jnp.where(causal, cum_c - cum_b, -1e30))
            scores = lax.dot_general(
                c_blk, b_blk, (((1,), (1,)), ((), ())), preferred_element_type=f32
            )
            mix = (scores * seg * step_ref[pl.ds(c, 1), :]).astype(bf16)
            ys.append(jnp.dot(mix, xc, preferred_element_type=f32))
            e_c = jnp.exp(cum_c)
            ecs.append(e_c)
            wcs.append(w_c)
            decays.append(e_c[span - 1 : span, :])
            bs.append(b_blk)
            cs.append(c_blk)
        scaled = (jnp.where(odd, wcs[1], wcs[0]) * xcf).astype(bf16)
        adds = [
            lax.dot_general(b, scaled, (((0,), (0,)), ((), ())), preferred_element_type=f32)
            for b in bs
        ]
        after_even = decays[0] * state + adds[0]
        entering = jnp.where(odd, pltpu.roll(after_even, HEAD_DIM, 1), state)
        ent_hi = entering.astype(bf16)
        ent_lo = (entering - ent_hi.astype(f32)).astype(bf16)
        outs = []
        for h in range(2):
            from_state = jnp.dot(cs[h], ent_hi, preferred_element_type=f32) + jnp.dot(
                cs[h], ent_lo, preferred_element_type=f32
            )
            outs.append(ys[h] + ecs[h] * from_state)
        y = jnp.where(odd, outs[1], outs[0]) + skip * xcf
        yl[i] = y.astype(bf16).reshape(n, sub, LANES)
        after_odd = decays[1] * entering + adds[1]
        s_ref[...] = pltpu.roll(after_odd, HEAD_DIM, 1)
        return carry

    lax.fori_loop(0, pairs, pair, 0)
    fin[...] = s_ref[...].T[0:HEAD_DIM, :]
    per = HEAD_DIM // n
    for u in range(per):
        v = fin[pl.ds(u, n, stride=per), :]
        slabs[:, u, :] = jnp.dot(
            eye.astype(f32), v, precision=highest, preferred_element_type=f32
        )

    def send_y(to, k):
        copy_to(yl.at[:, to], yg.at[me], y_send, y_recv.at[k], {"seq": to}).start()

    def send_lap(k, carry):
        p = pair_at(k)
        send_y(2 * p, k)
        send_y(2 * p + 1, k)
        return carry

    send_y(sibling, 0)
    lax.fori_loop(1, pairs, send_lap, 0)
    yg[me] = yl[:, me]

    def send_state(k, carry):
        to = lax.rem(me + k, n)
        copy_to(slabs.at[to], state_out.at[me], st_send, st_recv, {"seq": to}).start()
        return carry

    lax.fori_loop(1, n, send_state, 0)
    state_out[me] = slabs[me]

    for k in range(1, groups):
        from_grp = lax.rem(grp - k + groups, groups)
        arrived(wall.at[pl.ds(0, (n - 1) * part_rows)], wgrp_recv.at[k - 1], to_right)

        def pass_on(j, carry):
            block = wslot(lax.rem(me + j, n), from_grp)
            to_sibling(block, block)
            return carry

        lax.fori_loop(1, n, pass_on, 0)

    def unpack(p):
        lanes = pl.ds(pl.multiple_of(p * LANES, LANES), LANES)
        first = yg[2 * p].reshape(half, LANES).astype(f32)
        second = yg[2 * p + 1].reshape(half, LANES).astype(f32)
        for h, v in enumerate(swap_halves(first, second)):
            gate = gate_ref[:, h, :, lanes].reshape(half, LANES).astype(f32)
            gated = v * silu(gate)
            squares[h * half : (h + 1) * half, :] += gated * gated
            feat[g, p, h * half : (h + 1) * half, :] = (gated * gain_ref[:, lanes]).astype(bf16)

    def spread(p):
        for k in range(1, quarters):
            copy_to(
                feat.at[g, p], feat.at[g, p], f_send, f_recv.at[k - 1],
                {"head": lax.rem(g + k, quarters)},
            ).start()

    def from_pair(k):
        return lax.rem(my_pair - offset_of(k) + pairs, pairs)

    squares[...] = jnp.zeros(squares.shape, f32)
    arrived(yg.at[0], y_recv.at[0], to_right)
    unpack(my_pair)

    def y_lap(k, carry):
        arrived(yg.at[pl.ds(0, 2)], y_recv.at[k], to_right)
        unpack(from_pair(k))
        spread(from_pair(k - 1))
        return carry

    lax.fori_loop(1, pairs, y_lap, 0)
    total = jnp.broadcast_to(jnp.sum(squares[...], axis=1, keepdims=True), (rows, LANES))
    sums[g] = total.T[0:8, :]
    spread(from_pair(pairs - 1))
    for k in range(1, quarters):
        copy_to(
            sums.at[g], sums.at[g], q_send, q_recv.at[k - 1], {"head": lax.rem(g + k, quarters)}
        ).start()

    if reps == 2:
        arrived(wall.at[pl.ds(0, inner // 2)], wsib_recv, to_right)
    acc[...] = jnp.zeros(acc.shape, f32)
    group = 4 if pairs % 4 == 0 else 1

    def project(owner):
        def step_k(t, carry):
            first = t * group
            lhs = jnp.concatenate([feat[owner, first + u] for u in range(group)], axis=1)
            at = owner * (pairs * LANES) + first * LANES
            rhs = wall[pl.ds(pl.multiple_of(at, LANES), group * LANES), :]
            acc[...] += jnp.dot(lhs, rhs, preferred_element_type=f32)
            return carry

        lax.fori_loop(0, pairs // group, step_k, 0)

    project(g)
    for k in range(1, quarters):
        owner = lax.rem(g - k + quarters, quarters)
        arrived(feat.at[owner], f_recv.at[k - 1], to_right)
        arrived(sums.at[owner], q_recv.at[k - 1], to_right)
        project(owner)
    row_sum = sums[0]
    for k in range(1, quarters):
        row_sum = row_sum + sums[k]
    mean = jnp.broadcast_to(row_sum[0:1, :], (LANES, rows)).T * (1.0 / inner)
    scale = lax.rsqrt(mean + EPS)
    for q in range(cols // LANES):
        part = slice(q * LANES, (q + 1) * LANES)
        for h in range(2):
            here = slice(h * half, (h + 1) * half)
            block = (acc[here, part] * scale[here, :]).astype(bf16)
            ms[:, h, :, part] = block.reshape(pairs, sub, LANES)

    def send_m(k, carry):
        to = lax.rem(me + offset_of(k) + n, n)
        copy_to(
            ms.at[lax.div(to, 2), lax.rem(to, 2)], mg.at[me], m_send, m_recv, {"seq": to}
        ).start()
        return carry

    mg[me] = ms[my_pair, lax.rem(me, 2)]
    lax.fori_loop(1, n, send_m, 0)

    sent(xg.at[:, pl.ds(0, n - 1)], x_send, to_right)
    sent(dtg.at[pl.ds(0, n - 1)], dt_send, to_right)
    for k in range(1, quarters):
        sent(bcg.at[pl.ds(0, share)], side_send, to_right)
        sent(feat.at[0], f_send, to_right)
        sent(sums.at[0], q_send, to_right)

    def drain(k, carry):
        sent(slot(me), ring_send.at[0, k], to_right)
        sent(wslot(me, grp), wring_send.at[0, k], to_right)

        @pl.when(k < last_left)
        def _():
            sent(slot(me), ring_send.at[1, k], to_right)
            sent(wslot(me, grp), wring_send.at[1, k], to_right)

        return carry

    lax.fori_loop(0, last_right, drain, 0)
    if reps == 2:
        sent(wall.at[pl.ds(0, inner // 2)], wsib_send, to_right)
    for k in range(1, groups):
        sent(wall.at[pl.ds(0, (n - 1) * part_rows)], wgrp_send, to_right)
    sent(yg.at[pl.ds(0, n - 1)], y_send, to_right)
    sent(state_out.at[pl.ds(0, n - 1)], st_send, to_right)

    @pl.when(me == n - 1)
    def _():
        sent(tails.at[pl.ds(0, n - 1)], tail_send, to_right)

    @pl.when(me != n - 1)
    def _():
        arrived(tailx_out, tail_recv, to_right)

    arrived(state_out.at[pl.ds(0, n - 1)], st_recv, to_right)
    arrived(mg.at[pl.ds(0, n - 1)], m_recv, to_right)
    for q in range(cols // LANES):
        part = slice(q * LANES, (q + 1) * LANES)
        out_ref[:, part] = mg[:, :, part].reshape(n * sub, LANES)
    sent(mg.at[pl.ds(0, n - 1)], m_send, to_right)


def layer(start, a_rate, dt_bias, d_skip, owner, taps, wbc, gain, dt, bc, x, weight, gate, n, quarters):
    pairs, _, sub, width = x.shape
    blocks, span = 2 * pairs, n * sub
    piece, cols = weight.shape
    inner = width * quarters
    rows = blocks * sub
    per = HEAD_DIM // n
    dma = pltpu.SemaphoreType.DMA
    ring = dma((2, n // 2))
    return pl.pallas_call(
        layer_kernel,
        out_shape=(
            jax.ShapeDtypeStruct((span, cols), bf16),
            jax.ShapeDtypeStruct((n, per, LANES), f32),
            jax.ShapeDtypeStruct((sub, LANES), bf16),
            jax.ShapeDtypeStruct((sub, 2 * NSTATE), bf16),
        ),
        in_specs=[SM] * 4 + [VM] * 9,
        out_specs=(VM,) * 4,
        scratch_shapes=[
            pltpu.VMEM((n, pairs, sub, LANES), bf16),
            pltpu.VMEM((pairs, n, sub, LANES), bf16),
            pltpu.VMEM((n, 1, rows), f32),
            pltpu.VMEM((n, 1, rows), f32),
            pltpu.VMEM((blocks, n, sub, 2 * NSTATE), bf16),
            pltpu.VMEM((inner, cols), bf16),
            pltpu.VMEM((pairs, n, sub, LANES), bf16),
            pltpu.VMEM((n, pairs, sub, LANES), bf16),
            pltpu.VMEM((quarters, pairs, rows, LANES), bf16),
            pltpu.VMEM((rows, LANES), f32),
            pltpu.VMEM((quarters, 8, rows), f32),
            pltpu.VMEM((pairs, 2, sub, cols), bf16),
            pltpu.VMEM((n, sub, cols), bf16),
            pltpu.VMEM((rows, cols), f32),
            pltpu.VMEM((n, per, LANES), f32),
            pltpu.VMEM((n, sub, LANES), bf16),
            pltpu.VMEM((HEAD_DIM, NSTATE), f32),
            pltpu.VMEM((n * sub, LANES), f32),
            pltpu.VMEM((blocks, span), f32),
            pltpu.VMEM((blocks, span), f32),
            pltpu.VMEM((blocks, span), f32),
            pltpu.VMEM((8 + span, LANES), f32),
            pltpu.VMEM((8 + 2 * span, 2 * NSTATE), f32),
            pltpu.VMEM((2 * span, 2 * NSTATE), bf16),
            pltpu.VMEM((NSTATE, LANES), f32),
            dma, dma, dma, dma, ring, ring, dma, dma((4,)),
            ring, ring, dma, dma, dma, dma((8,)),
            dma, dma, dma, dma((pairs,)), dma, dma, dma, dma((4,)), dma, dma((4,)),
            dma, dma,
        ],
        compiler_params=pltpu.CompilerParams(
            collective_id=1, has_side_effects=True, vmem_limit_bytes=48 * 1024 * 1024
        ),
        cost_estimate=pl.CostEstimate(
            flops=2_000_000_000, bytes_accessed=300_000_000, transcendentals=4_000_000
        ),
        name="layer",
    )(start, a_rate, dt_bias, d_skip, owner, taps, wbc, gain, dt, bc, x, weight, gate)


def local(
    x_proj, gate_proj, bc_proj, dt_proj, a_rate, dt_bias, d_skip,
    conv_x_weight, conv_bc_weight, norm_gain, out_weight, request_first_position, owner,
):
    _, blocks, _, sub, width = x_proj.shape
    n, quarters = lax.axis_size("seq"), lax.axis_size("head")
    me = lax.axis_index("seq")
    pairs = blocks // 2
    start = request_first_position
    mixed, state, tail_x, tail_bc = layer(
        start, a_rate, dt_bias, d_skip, owner, conv_x_weight, conv_bc_weight, norm_gain[None],
        dt_proj.reshape(blocks, sub, n), bc_proj.reshape(blocks, sub, 2 * NSTATE),
        x_proj.reshape(pairs, 2, sub, width), out_weight,
        gate_proj.reshape(pairs, 2, sub, width), n, quarters,
    )
    keep = KCONV - 1
    conv_x_state = tail_x[sub - keep :, HEAD_DIM:][None, None]
    my_slab = jnp.sum(jnp.where(owner[0] == me, jnp.arange(n, dtype=jnp.int32), 0))
    positions = blocks * n * sub - keep + jnp.arange(keep, dtype=jnp.int32)
    tail_bc = jnp.where(
        (positions >= start[0])[:, None], tail_bc[sub - keep :], jnp.zeros((), bf16)
    )
    conv_bc_state = lax.dynamic_index_in_dim(
        tail_bc.reshape(keep, n, -1), my_slab, axis=1, keepdims=False
    )[None, None]
    return (mixed[None], state.reshape(1, 1, n, -1), conv_x_state, conv_bc_state)


def solution(mesh):
    return jax.shard_map(
        local,
        mesh=mesh,
        in_specs=(
            P(("grp", "rep"), None, "seq", None, "head"),
            P(("grp", "rep"), None, "seq", None, "head"),
            P(("grp", "rep"), None, "seq", None, None),
            P(("grp", "rep"), None, "seq", None, "head"),
            P("head"),
            P("head"),
            P("head"),
            P(None, "head"),
            P(),
            P("head"),
            P(("seq", "rep"), "head"),
            P(("grp", "rep")),
            P(("grp", "rep"), None),
        ),
        out_specs=(
            P(("grp", "rep"), "seq", "head"),
            P(("grp", "rep"), "seq", "head", None),
            P(("grp", "rep"), "seq", None, "head"),
            P(("grp", "rep"), "seq", None, None),
        ),
        check_vma=False,
    )
```

time: 555 us -> 251 us (0.45)
  waiting for transfers between devices: 389 us -> 0 us
  Pallas kernels: 13 us -> 236 us
  starting transfers between devices: 71.7 us -> 0 us
  local copies, waits for them, and re-layouts: 35.9 us -> 9.26 us
  between operations: 16.8 us -> 3.33 us
  blocking collectives: 11.5 us -> 0 us
  other arithmetic: 9.79 us -> 0.71 us
    all_gather x3 -> x0, waiting for transfers between devices: 316 us -> none  [the longest x1 146 us: local(): bc_all = lax.all_gather(bc_proj.reshape(blocks, sub, 2 * NSTATE), 'seq')]
    pallas_call x1, Pallas kernels: 13 us -> 236 us  [layer(): pl.pallas_call(layer_kernel, out_shape=(jax.ShapeDtypeStruct((span, cols)...]
    all_to_all x3 -> x0, waiting for transfers between devices: 72.4 us -> none  [exchange(): return lax.all_to_all(value, axis, split_axis=0, concat_axis=0, tiled=True)]
    all_to_all x3 -> x0, starting transfers between devices: 71.3 us -> none  [exchange(): return lax.all_to_all(value, axis, split_axis=0, concat_axis=0, tiled=True)]
    convert_element_type x5 -> x0, local copies, waits for them, and re-layouts: 11.9 us -> none  [the longest x3 8.75 us: local(): gated = y_mine.astype(f32) * jax.nn.silu(gate)]
    psum x1 -> x0, blocking collectives: 11.5 us -> none  [local(): squares = lax.psum(jnp.sum(gated * gated, axis=1), 'head')]
    reshape x11 -> x2, local copies, waits for them, and re-layouts: 8.69 us -> 0.74 us  [the longest x1 0.64 us: local(): state.reshape(1, 1, n, -1)]
    unnamed x26, local copies, waits for them, and re-layouts: 1.34 us -> 7.88 us
  transfers between devices with their start and end apart: 6 -> 0, of which waited for: 5 -> 0; matrix products, arithmetic and copies ran while one was open for 3% -> 0% of each run, Pallas kernels for 0% -> 0%
where the time goes in v3:
time: 251 us; the launch traced here: 249 us
  Pallas kernels  236 us (94%)
  local copies, waits for them, and re-layouts  9.26 us (4%)
  between operations  3.33 us (1%)
    pallas_call x1, Pallas kernels, layer(): pl.pallas_call(layer_kernel, out_shape=(jax.ShapeDtypeStruct((span, cols)...  236 us
    unnamed x26, local copies, waits for them, and re-layouts  7.88 us

profile of v3, /device:TPU:40, one launch (start us, length us, event | category | flops | bytes accessed | tf_op | source)
XLA Modules:
  0.0 249.2 jit_solution(13175294764816722450)
XLA Ops:
  0.6 0.0 copy-start.11
  0.6 0.6 copy-done.11
  1.3 0.6 fusion
  2.6 0.0 copy-start.6
  4.5 0.0 copy-start.7
  4.6 0.0 copy-start.8
  4.6 0.0 copy-start.9
  4.6 0.0 copy-start.10
  4.6 0.0 copy-done.6
  4.6 0.6 copy-done.7
  5.2 0.0 copy-done.8
  5.2 0.0 copy-done.9
  5.2 0.0 copy-done.10
  5.2 0.0 copy-start
  5.2 1.0 copy-done
  6.3 0.0 copy-start.1
  6.3 1.0 copy-done.1
  7.3 0.0 copy-start.2
  7.3 0.9 copy-done.2
  8.2 0.0 copy-start.3
  8.2 0.8 copy-done.3
  9.1 0.0 copy-start.4
  9.1 0.8 copy-done.4
  9.8 0.0 copy-start.5
  9.8 0.8 copy-done.5
  10.6 235.9 %layer.1 = (bf16[128,512]{1,0:T(8,128)(2,1)S(1)}, f32[32,2,128]{2,1,0:T(2,128)S(1)}, bf16[4,128]{1,0:T(4,128)(2,1)S(1)}, bf16[4,256]{1,0:T(4,128)(2,1)S(1)}) custom-call(s32[1]{0:T(128)} %copy.22.start_ref, f32[32]{0:T(128)S(1)} %copy-done.8, f32[32]{0:T(128)S(1)} %copy-done.9, f32[32]{0:T(128)S(1)} %copy-done.10, s32[1,32]{1,0:T(1,128)S(1)} %copy-done.11, ...), custom_call_target="tpu_custom_call" | custom-call | flops 2000000000 | bytes 300000000 | tf_op jit(solution)/shard_map/layer/pallas_call | solution.py:529
  246.6 0.1 slice_select_fusion
  246.6 0.1 reshape.39
  246.8 0.6 copy.20
  247.3 0.6 reshape.38
  248.0 0.6 slice_bitcast_fusion
  248.6 0.7 copy.23
  (2 shorter events, 0.0 us)
Async XLA Ops:
  0.6 0.7 copy-start.11
  2.6 2.0 copy-start.6
  4.5 0.7 copy-start.7
  4.6 0.7 copy-start.8
  4.6 0.7 copy-start.9
  4.6 0.7 copy-start.10
  5.2 1.0 copy-start
  6.3 1.0 copy-start.1
  7.3 0.9 copy-start.2
  8.2 0.8 copy-start.3
  9.1 0.8 copy-start.4
  9.8 0.8 copy-start.5

commit v4 on v3

--- a/solution.py
+++ b/solution.py
@@ -15,6 +15,7 @@
 MESH = pl.DeviceIdType.MESH
 VM = pl.BlockSpec(memory_space=pltpu.VMEM)
 SM = pl.BlockSpec(memory_space=pltpu.SMEM)
+HBM = pl.BlockSpec(memory_space=pltpu.HBM)
 
 highest = lax.Precision.HIGHEST
 f32, bf16 = jnp.float32, jnp.bfloat16
@@ -74,15 +75,16 @@
 
 
 def layer_kernel(
-    start_ref, a_ref, bias_ref, skip_ref, owner_ref, taps_ref, wbc_ref, gain_ref,
-    dt_ref, bc_ref, x_ref, w_ref, gate_ref,
+    start_ref, a_ref, bias_ref, skip_ref, owner_hbm, taps_hbm, wbc_hbm, gain_hbm,
+    dt_hbm, bc_hbm, x_hbm, w_hbm, gate_hbm,
     out_ref, state_out, tailx_out, tailbc_out,
+    owner_ref, taps_ref, wbc_ref, gain_ref, dt_ref, bc_ref, x_ref, w_ref, gate_ref,
     xs, xg, dts, dtg, bcg, wall, yl, yg, feat, squares, sums, ms, mg, acc, slabs, tails, fin, wide,
     cum_ref, wgt_ref, step_ref, extx_ref, extbc_ref, bc_conv_ref, s_ref,
     x_send, x_recv, dt_send, dt_recv, ring_send, ring_recv, side_send, side_recv,
     wring_send, wring_recv, wsib_send, wsib_recv, wgrp_send, wgrp_recv,
     tail_send, tail_recv, y_send, y_recv, st_send, st_recv, f_send, f_recv, q_send, q_recv,
-    m_send, m_recv,
+    m_send, m_recv, load_sem,
 ):
     pairs, _, sub, _ = x_ref.shape
     blocks = 2 * pairs
@@ -106,7 +108,16 @@
     part_rows = piece // groups
     start = start_ref[0]
 
+    sources = (bc_hbm, w_hbm, x_hbm, dt_hbm, owner_hbm, taps_hbm, wbc_hbm, gain_hbm, gate_hbm)
+    places = (bc_ref, w_ref, x_ref, dt_ref, owner_ref, taps_ref, wbc_ref, gain_ref, gate_ref)
+    loads = [
+        pltpu.make_async_copy(a, b, load_sem.at[i]) for i, (a, b) in enumerate(zip(sources, places))
+    ]
+    for load in loads:
+        load.start()
     greet(("seq", "head", "rep", "grp"))
+    loads[0].wait()
+    loads[1].wait()
 
     def slot(owner):
         return bcg.at[pl.ds(g * share, share), owner]
@@ -115,11 +126,53 @@
         at = (owner * reps + rep) * piece + which * part_rows
         return wall.at[pl.ds(pl.multiple_of(at, 16), part_rows)]
 
-    def ring(src, wsrc, owner, step, way):
-        there = {"seq": right if way == 0 else left}
-        copy_to(src, slot(owner), ring_send.at[way, step], ring_recv.at[way, step], there).start()
+    def onward(way):
+        return {"seq": right if way == 0 else left}
+
+    half_share = share // 2
+
+    def half_slot(owner, way):
+        return bcg.at[pl.ds(g * share + way * half_share, half_share), owner]
+
+    def spread_bc(t):
+        by = n >> (t + 1)
+        for way in range(2):
+            sign = 1 - 2 * way
+            to = {"seq": lax.rem(me + sign * by + n, n)}
+            own = bc_ref.at[pl.ds(g * share + way * half_share, half_share)]
+            copy_to(own, half_slot(me, way), ring_send, ring_recv.at[way, t], to).start()
+
+            def give(m, carry):
+                owner = lax.rem(me - sign * (2 * by) * m + n, n)
+                block = half_slot(owner, way)
+                copy_to(block, block, ring_send, ring_recv.at[way, t], to).start()
+                return carry
+
+            lax.fori_loop(1, 1 << t, give, 0)
+
+    def take_bc(t):
+        by = n >> (t + 1)
+        for way in range(2):
+            sign = 1 - 2 * way
+            arrived(
+                bcg.at[pl.ds(0, half_share), pl.ds(0, 1 << t)], ring_recv.at[way, t], to_right
+            )
+
+            def give(m, carry):
+                owner = lax.rem(me - sign * by * (2 * m + 1) + n, n)
+                block = half_slot(owner, way)
+                for k in range(1, quarters):
+                    copy_to(
+                        block, block, side_send, side_recv.at[k - 1],
+                        {"head": lax.rem(g + k, quarters)},
+                    ).start()
+                return carry
+
+            lax.fori_loop(0, 1 << t, give, 0)
+
+    def wring(src, owner, step, way):
         copy_to(
-            wsrc, wslot(owner, grp), wring_send.at[way, step], wring_recv.at[way, step], there
+            src, wslot(owner, grp), wring_send.at[way, step], wring_recv.at[way, step], onward(way)
         ).start()
 
     def aside(src, owner):
@@ -133,19 +186,62 @@
         if reps == 2:
             copy_to(src, dst, wsib_send, wsib_recv, {"rep": 1 - rep}).start()
 
-    def hand_on(owner):
+    def hand_on(owner, late):
         block = wslot(owner, grp)
         to_sibling(block, block)
         for k in range(1, groups):
             copy_to(
-                block, block, wgrp_send, wgrp_recv.at[k - 1], {"grp": lax.rem(grp + k, groups)}
+                block, block, wgrp_send, wgrp_recv.at[k - 1, late],
+                {"grp": lax.rem(grp + k, groups)},
             ).start()
+
+    laps = last_right - 1
+
+    def w_lap(j, late):
+        from_left, from_right = lax.rem(me - j + n, n), lax.rem(me + j, n)
+        arrived(wslot(from_left, grp), wring_recv.at[0, j - 1], to_right)
+        wring(wslot(from_left, grp), from_left, j, 0)
+        hand_on(from_left, late)
+        arrived(wslot(from_right, grp), wring_recv.at[1, j - 1], to_right)
+
+        @pl.when(j < last_left)
+        def _():
+            wring(wslot(from_right, grp), from_right, j, 1)
+
+        hand_on(from_right, late)
+
+    def w_end():
+        far = lax.rem(me + n - last_right, n)
+        arrived(wslot(far, grp), wring_recv.at[0, last_right - 1], to_right)
+        hand_on(far, 1)
+
+    def pass_on(first, last, late):
+        if reps != 2 and groups == 1:
+            return
+        both = 2 * (last - first + 1) - (1 if late else 0)
+        for k in range(1, groups):
+            from_grp = lax.rem(grp - k + groups, groups)
+            arrived(wall.at[pl.ds(0, both * part_rows)], wgrp_recv.at[k - 1, late], to_right)
+
+            def give(j, carry):
+                block = wslot(lax.rem(me - j + n, n), from_grp)
+                to_sibling(block, block)
+
+                @pl.when(j < last_right)
+                def _():
+                    other = wslot(lax.rem(me + j, n), from_grp)
+                    to_sibling(other, other)
+
+                return carry
+
+            lax.fori_loop(first, last + 1, give, 0)
 
     own_rows = pl.ds(pl.multiple_of((me * reps + rep) * piece, 16), piece)
     own_part = w_ref.at[pl.ds(pl.multiple_of(grp * part_rows, 16), part_rows)]
-    ring(mine, own_part, me, 0, 0)
-    ring(mine, own_part, me, 0, 1)
+    spread_bc(0)
     aside(mine, me)
+    wring(own_part, me, 0, 0)
+    wring(own_part, me, 0, 1)
     to_sibling(w_ref, wall.at[own_rows])
     bcg[pl.ds(g * share, share), me] = bc_ref[pl.ds(g * share, share)]
     wall[own_rows, :] = w_ref[...]
@@ -164,40 +260,27 @@
     def pair_at(k):
         return lax.rem(my_pair + offset_of(k) + pairs, pairs)
 
+    loads[2].wait()
+    loads[3].wait()
     pack(my_pair)
-    pack(pair_at(1))
+    pack(pair_at(pairs - 1))
     send_x(sibling)
     xg[:, me] = xs[me]
     dt_t = dt_ref[...].astype(f32).reshape(blocks * sub, n).T
     dts[...] = dt_t.reshape(n, 1, blocks * sub)
 
-    def lap(k, carry):
-        @pl.when(k + 1 < pairs)
+    def x_lap(k, carry):
+        @pl.when(k > 1)
         def _():
-            pack(pair_at(k + 1))
-
-        @pl.when(k < pairs)
-        def _():
-            p = pair_at(k)
-            send_x(2 * p)
-            send_x(2 * p + 1)
-
-        from_left, from_right = lax.rem(me - k + n, n), lax.rem(me + k, n)
-        arrived(slot(from_left), ring_recv.at[0, k - 1], to_right)
-        arrived(wslot(from_left, grp), wring_recv.at[0, k - 1], to_right)
-        ring(slot(from_left), wslot(from_left, grp), from_left, k, 0)
-        aside(slot(from_left), from_left)
-        hand_on(from_left)
-        arrived(slot(from_right), ring_recv.at[1, k - 1], to_right)
-        arrived(wslot(from_right, grp), wring_recv.at[1, k - 1], to_right)
-
-        @pl.when(k < last_left)
-        def _():
-            ring(slot(from_right), wslot(from_right, grp), from_right, k, 1)
-
-        aside(slot(from_right), from_right)
-        hand_on(from_right)
-        return carry
+            pack(pair_at(k - 1))
+
+        p = pair_at(k)
+        send_x(2 * p)
+        send_x(2 * p + 1)
+        return carry
+
+    def x_pairs(last, first):
+        lax.fori_loop(0, last - first, lambda u, c: x_lap(last - 1 - u, c), 0)
 
     def dt_out(k, carry):
         to = lax.rem(me + offset_of(k) + n, n)
@@ -206,12 +289,30 @@
 
     lax.fori_loop(1, n, dt_out, 0)
     dtg[me] = dts[me]
-    lax.fori_loop(1, last_right, lap, 0)
-    far = lax.rem(me + n - last_right, n)
-    arrived(slot(far), ring_recv.at[0, last_right - 1], to_right)
-    arrived(wslot(far, grp), wring_recv.at[0, last_right - 1], to_right)
-    aside(slot(far), far)
-    hand_on(far)
+    steps = n.bit_length() - 1
+    ends = [1 + (pairs - 1) * w // 16 for w in (14, 12, 10, 8, 7)][:steps]
+    ends += [1] * (steps - len(ends))
+    upto_pair = pairs
+    done = 0
+    for t in range(steps):
+        x_pairs(upto_pair, ends[t])
+        upto_pair = ends[t]
+        goal = 4 * laps * (t + 1) // (5 * steps)
+        if done < goal:
+            done += 1
+            w_lap(done, 1)
+        take_bc(t)
+        if t + 1 < steps:
+            spread_bc(t + 1)
+        while done < goal:
+            done += 1
+            w_lap(done, 1)
+    x_pairs(upto_pair, 1)
+    for j in range(done + 1, laps + 1):
+        w_lap(j, 1)
+    w_end()
+    for load in loads[4:]:
+        load.wait()
 
     eye = lax.broadcasted_iota(jnp.int32, (n, n), 0) == owner_ref[...]
     chosen = eye.astype(bf16)
@@ -226,9 +327,6 @@
 
     arrived(xg.at[:, pl.ds(0, n - 1)], x_recv, to_right)
     arrived(dtg.at[pl.ds(0, n - 1)], dt_recv, to_right)
-    for k in range(1, quarters):
-        from_g = lax.rem(g - k + quarters, quarters)
-        arrived(bcg.at[pl.ds(from_g * share, share)], side_recv.at[k - 1], to_right)
 
     @pl.when(me == n - 1)
     def _():
@@ -240,7 +338,6 @@
         lax.fori_loop(1, n, send_tail, 0)
         tailx_out[...] = tails[n - 1]
 
-    tailbc_out[...] = bcg[blocks - 1, n - 1]
 
     row = lax.broadcasted_iota(jnp.int32, (span, LANES), 0)
     lane = lax.broadcasted_iota(jnp.int32, (span, LANES), 1)
@@ -283,7 +380,7 @@
     causal = row >= lane
     odd8 = lax.broadcasted_iota(jnp.int32, (8, LANES), 1) >= HEAD_DIM
 
-    def pair(i, carry):
+    def convolve_x(i, carry):
         base = i * (2 * span)
         live_x = (base + jnp.where(odd, span, 0) + row) >= start
         xf = jnp.where(live_x, xg[i].reshape(span, LANES).astype(f32), 0.0)
@@ -294,7 +391,27 @@
         for k in range(KCONV):
             acc = acc + taps[k : k + 1, :] * extx_ref[pl.ds(8 - (KCONV - 1) + k, span), :]
         extx_ref[0:8, :] = last
-        xc = silu(acc).astype(bf16)
+        xg[i] = silu(acc).astype(bf16).reshape(n, sub, LANES)
+        return carry
+
+    lax.fori_loop(0, pairs, convolve_x, 0)
+    for k in range(1, quarters):
+        from_g = lax.rem(g - k + quarters, quarters)
+        arrived(bcg.at[pl.ds(from_g * share, share)], side_recv.at[k - 1], to_right)
+    tailbc_out[...] = bcg[blocks - 1, n - 1]
+
+    def send_y(to, k):
+        copy_to(yl.at[:, to], yg.at[me], y_send, y_recv.at[k], {"seq": to}).start()
+
+    def send_lap(k, carry):
+        p = pair_at(k)
+        send_y(2 * p, k)
+        send_y(2 * p + 1, k)
+        return carry
+
+    def pair(i, carry):
+        base = i * (2 * span)
+        xc = xg[i].reshape(span, LANES)
         xcf = xc.astype(f32)
 
         rows1 = lax.broadcasted_iota(jnp.int32, (span, 2 * NSTATE), 0)
@@ -360,15 +477,6 @@
             eye.astype(f32), v, precision=highest, preferred_element_type=f32
         )
 
-    def send_y(to, k):
-        copy_to(yl.at[:, to], yg.at[me], y_send, y_recv.at[k], {"seq": to}).start()
-
-    def send_lap(k, carry):
-        p = pair_at(k)
-        send_y(2 * p, k)
-        send_y(2 * p + 1, k)
-        return carry
-
     send_y(sibling, 0)
     lax.fori_loop(1, pairs, send_lap, 0)
     yg[me] = yl[:, me]
@@ -381,16 +489,7 @@
     lax.fori_loop(1, n, send_state, 0)
     state_out[me] = slabs[me]
 
-    for k in range(1, groups):
-        from_grp = lax.rem(grp - k + groups, groups)
-        arrived(wall.at[pl.ds(0, (n - 1) * part_rows)], wgrp_recv.at[k - 1], to_right)
-
-        def pass_on(j, carry):
-            block = wslot(lax.rem(me + j, n), from_grp)
-            to_sibling(block, block)
-            return carry
-
-        lax.fori_loop(1, n, pass_on, 0)
+    pass_on(1, last_right, 1)
 
     def unpack(p):
         lanes = pl.ds(pl.multiple_of(p * LANES, LANES), LANES)
@@ -413,8 +512,6 @@
         return lax.rem(my_pair - offset_of(k) + pairs, pairs)
 
     squares[...] = jnp.zeros(squares.shape, f32)
-    arrived(yg.at[0], y_recv.at[0], to_right)
-    unpack(my_pair)
 
     def y_lap(k, carry):
         arrived(yg.at[pl.ds(0, 2)], y_recv.at[k], to_right)
@@ -422,6 +519,8 @@
         spread(from_pair(k - 1))
         return carry
 
+    arrived(yg.at[0], y_recv.at[0], to_right)
+    unpack(my_pair)
     lax.fori_loop(1, pairs, y_lap, 0)
     total = jnp.broadcast_to(jnp.sum(squares[...], axis=1, keepdims=True), (rows, LANES))
     sums[g] = total.T[0:8, :]
@@ -466,7 +565,7 @@
             ms[:, h, :, part] = block.reshape(pairs, sub, LANES)
 
     def send_m(k, carry):
-        to = lax.rem(me + offset_of(k) + n, n)
+        to = lax.rem(me + offset_of(n - k) + n, n)
         copy_to(
             ms.at[lax.div(to, 2), lax.rem(to, 2)], mg.at[me], m_send, m_recv, {"seq": to}
         ).start()
@@ -483,17 +582,16 @@
         sent(sums.at[0], q_send, to_right)
 
     def drain(k, carry):
-        sent(slot(me), ring_send.at[0, k], to_right)
         sent(wslot(me, grp), wring_send.at[0, k], to_right)
 
         @pl.when(k < last_left)
         def _():
-            sent(slot(me), ring_send.at[1, k], to_right)
             sent(wslot(me, grp), wring_send.at[1, k], to_right)
 
         return carry
 
     lax.fori_loop(0, last_right, drain, 0)
+    sent(bcg.at[pl.ds(0, share), pl.ds(0, n - 1)], ring_send, to_right)
     if reps == 2:
         sent(wall.at[pl.ds(0, inner // 2)], wsib_send, to_right)
     for k in range(1, groups):
@@ -534,9 +632,10 @@
             jax.ShapeDtypeStruct((sub, LANES), bf16),
             jax.ShapeDtypeStruct((sub, 2 * NSTATE), bf16),
         ),
-        in_specs=[SM] * 4 + [VM] * 9,
+        in_specs=[SM] * 4 + [HBM] * 9,
         out_specs=(VM,) * 4,
         scratch_shapes=[
+            *(pltpu.VMEM(v.shape, v.dtype) for v in (owner, taps, wbc, gain, dt, bc, x, weight, gate)),
             pltpu.VMEM((n, pairs, sub, LANES), bf16),
             pltpu.VMEM((pairs, n, sub, LANES), bf16),
             pltpu.VMEM((n, 1, rows), f32),
@@ -562,13 +661,13 @@
             pltpu.VMEM((8 + 2 * span, 2 * NSTATE), f32),
             pltpu.VMEM((2 * span, 2 * NSTATE), bf16),
             pltpu.VMEM((NSTATE, LANES), f32),
-            dma, dma, dma, dma, ring, ring, dma, dma((4,)),
-            ring, ring, dma, dma, dma, dma((8,)),
+            dma, dma, dma, dma, dma, dma((2, n.bit_length())), dma, dma((4,)),
+            ring, ring, dma, dma, dma, dma((8, 2)),
             dma, dma, dma, dma((pairs,)), dma, dma, dma, dma((4,)), dma, dma((4,)),
-            dma, dma,
+            dma, dma, dma((9,)),
         ],
         compiler_params=pltpu.CompilerParams(
-            collective_id=1, has_side_effects=True, vmem_limit_bytes=48 * 1024 * 1024
+            collective_id=1, has_side_effects=True, vmem_limit_bytes=63 * 1024 * 1024
         ),
         cost_estimate=pl.CostEstimate(
             flops=2_000_000_000, bytes_accessed=300_000_000, transcendentals=4_000_000

time: 251 us -> 256 us (1.020)
  Pallas kernels: 236 us -> 246 us
  local copies, waits for them, and re-layouts: 9.26 us -> 4.79 us
    pallas_call x1, Pallas kernels: 236 us -> 246 us  [layer(): pl.pallas_call(layer_kernel, out_shape=(jax.ShapeDtypeStruct((span, cols)...]
    unnamed x26 -> x8, local copies, waits for them, and re-layouts: 7.88 us -> 3.4 us
where the time goes in v4:
time: 256 us; the launch traced here: 255 us
  Pallas kernels  246 us (96%)
  local copies, waits for them, and re-layouts  4.79 us (2%)
  between operations  3.27 us (1%)
    pallas_call x1, Pallas kernels, layer(): pl.pallas_call(layer_kernel, out_shape=(jax.ShapeDtypeStruct((span, cols)...  246 us

profile of v4, /device:TPU:40, one launch (start us, length us, event | category | flops | bytes accessed | tf_op | source)
XLA Modules:
  0.0 255.3 jit_solution(4126121463138550045)
XLA Ops:
  0.6 0.0 copy-start.2
  0.6 0.6 copy-done.2
  1.3 0.6 fusion
  4.5 245.9 %layer.1 = (bf16[128,512]{1,0:T(8,128)(2,1)}, f32[32,2,128]{2,1,0:T(2,128)}, bf16[4,128]{1,0:T(4,128)(2,1)}, bf16[4,256]{1,0:T(4,128)(2,1)}) custom-call(s32[1]{0:T(128)} %copy.22.start_ref, f32[32]{0:T(128)} %a_ref.1, f32[32]{0:T(128)} %bias_ref.1, f32[32]{0:T(128)} %skip_ref.1, s32[1,32]{1,0:T(1,128)} %owner_hbm.1, f32[4,2048]{1,0:T(4,128)} %taps_hbm.1, ...), custom_call_target="tpu_custom_call" | custom-call | flops 2000000000 | bytes 300000000 | tf_op jit(solution)/shard_map/layer/pallas_call | solution.py:627
  250.4 0.0 copy-start
  250.4 0.7 slice_select_fusion
  251.1 0.1 reshape.39
  251.3 0.6 copy.20
  251.8 0.0 copy-done
  251.8 0.6 reshape.38
  252.5 0.0 copy-start.1
  252.5 0.6 copy-done.1
  253.1 0.6 slice_bitcast_fusion
  253.7 1.6 copy.23
  (2 shorter events, 0.0 us)
Async XLA Ops:
  0.6 0.7 copy-start.2
  250.4 1.5 copy-start
  252.5 0.6 copy-start.1

commit v5 on v3

--- a/solution.py
+++ b/solution.py
@@ -15,6 +15,7 @@
 MESH = pl.DeviceIdType.MESH
 VM = pl.BlockSpec(memory_space=pltpu.VMEM)
 SM = pl.BlockSpec(memory_space=pltpu.SMEM)
+HBM = pl.BlockSpec(memory_space=pltpu.HBM)
 
 highest = lax.Precision.HIGHEST
 f32, bf16 = jnp.float32, jnp.bfloat16
@@ -74,15 +75,16 @@
 
 
 def layer_kernel(
-    start_ref, a_ref, bias_ref, skip_ref, owner_ref, taps_ref, wbc_ref, gain_ref,
-    dt_ref, bc_ref, x_ref, w_ref, gate_ref,
+    start_ref, a_ref, bias_ref, skip_ref, owner_hbm, taps_hbm, wbc_hbm, gain_hbm,
+    dt_hbm, bc_hbm, x_hbm, w_hbm, gate_hbm,
     out_ref, state_out, tailx_out, tailbc_out,
+    owner_ref, taps_ref, wbc_ref, gain_ref, dt_ref, bc_ref, x_ref, w_ref, gate_ref,
     xs, xg, dts, dtg, bcg, wall, yl, yg, feat, squares, sums, ms, mg, acc, slabs, tails, fin, wide,
     cum_ref, wgt_ref, step_ref, extx_ref, extbc_ref, bc_conv_ref, s_ref,
     x_send, x_recv, dt_send, dt_recv, ring_send, ring_recv, side_send, side_recv,
     wring_send, wring_recv, wsib_send, wsib_recv, wgrp_send, wgrp_recv,
     tail_send, tail_recv, y_send, y_recv, st_send, st_recv, f_send, f_recv, q_send, q_recv,
-    m_send, m_recv,
+    m_send, m_recv, load_sem,
 ):
     pairs, _, sub, _ = x_ref.shape
     blocks = 2 * pairs
@@ -106,7 +108,16 @@
     part_rows = piece // groups
     start = start_ref[0]
 
+    sources = (bc_hbm, w_hbm, x_hbm, dt_hbm, owner_hbm, taps_hbm, wbc_hbm, gain_hbm, gate_hbm)
+    places = (bc_ref, w_ref, x_ref, dt_ref, owner_ref, taps_ref, wbc_ref, gain_ref, gate_ref)
+    loads = [
+        pltpu.make_async_copy(a, b, load_sem.at[i]) for i, (a, b) in enumerate(zip(sources, places))
+    ]
+    for load in loads:
+        load.start()
     greet(("seq", "head", "rep", "grp"))
+    loads[0].wait()
+    loads[1].wait()
 
     def slot(owner):
         return bcg.at[pl.ds(g * share, share), owner]
@@ -164,6 +175,8 @@
     def pair_at(k):
         return lax.rem(my_pair + offset_of(k) + pairs, pairs)
 
+    loads[2].wait()
+    loads[3].wait()
     pack(my_pair)
     pack(pair_at(1))
     send_x(sibling)
@@ -212,6 +225,9 @@
     arrived(wslot(far, grp), wring_recv.at[0, last_right - 1], to_right)
     aside(slot(far), far)
     hand_on(far)
+
+    for load in loads[4:]:
+        load.wait()
 
     eye = lax.broadcasted_iota(jnp.int32, (n, n), 0) == owner_ref[...]
     chosen = eye.astype(bf16)
@@ -534,9 +550,10 @@
             jax.ShapeDtypeStruct((sub, LANES), bf16),
             jax.ShapeDtypeStruct((sub, 2 * NSTATE), bf16),
         ),
-        in_specs=[SM] * 4 + [VM] * 9,
+        in_specs=[SM] * 4 + [HBM] * 9,
         out_specs=(VM,) * 4,
         scratch_shapes=[
+            *(pltpu.VMEM(v.shape, v.dtype) for v in (owner, taps, wbc, gain, dt, bc, x, weight, gate)),
             pltpu.VMEM((n, pairs, sub, LANES), bf16),
             pltpu.VMEM((pairs, n, sub, LANES), bf16),
             pltpu.VMEM((n, 1, rows), f32),
@@ -565,10 +582,10 @@
             dma, dma, dma, dma, ring, ring, dma, dma((4,)),
             ring, ring, dma, dma, dma, dma((8,)),
             dma, dma, dma, dma((pairs,)), dma, dma, dma, dma((4,)), dma, dma((4,)),
-            dma, dma,
+            dma, dma, dma((9,)),
         ],
         compiler_params=pltpu.CompilerParams(
-            collective_id=1, has_side_effects=True, vmem_limit_bytes=48 * 1024 * 1024
+            collective_id=1, has_side_effects=True, vmem_limit_bytes=63 * 1024 * 1024
         ),
         cost_estimate=pl.CostEstimate(
             flops=2_000_000_000, bytes_accessed=300_000_000, transcendentals=4_000_000

time: 251 us -> 248 us (0.988)
  local copies, waits for them, and re-layouts: 9.26 us -> 4.79 us
    unnamed x26 -> x8, local copies, waits for them, and re-layouts: 7.88 us -> 3.4 us
where the time goes in v5:
time: 248 us; the launch traced here: 247 us
  Pallas kernels  238 us (96%)
  local copies, waits for them, and re-layouts  4.79 us (2%)
  between operations  3.27 us (1%)
    pallas_call x1, Pallas kernels, layer(): pl.pallas_call(layer_kernel, out_shape=(jax.ShapeDtypeStruct((span, cols)...  238 us

profile of v5, /device:TPU:40, one launch (start us, length us, event | category | flops | bytes accessed | tf_op | source)
XLA Modules:
  0.0 247.1 jit_solution(18001974191600572714)
XLA Ops:
  0.6 0.0 copy-start.2
  0.6 0.6 copy-done.2
  1.3 0.6 fusion
  4.5 237.6 %layer.1 = (bf16[128,512]{1,0:T(8,128)(2,1)}, f32[32,2,128]{2,1,0:T(2,128)}, bf16[4,128]{1,0:T(4,128)(2,1)}, bf16[4,256]{1,0:T(4,128)(2,1)}) custom-call(s32[1]{0:T(128)} %copy.22.start_ref, f32[32]{0:T(128)} %a_ref.1, f32[32]{0:T(128)} %bias_ref.1, f32[32]{0:T(128)} %skip_ref.1, s32[1,32]{1,0:T(1,128)} %owner_hbm.1, f32[4,2048]{1,0:T(4,128)} %taps_hbm.1, ...), custom_call_target="tpu_custom_call" | custom-call | flops 2000000000 | bytes 300000000 | tf_op jit(solution)/shard_map/layer/pallas_call | solution.py:545
  242.1 0.0 copy-start
  242.2 0.7 slice_select_fusion
  242.9 0.1 reshape.39
  243.0 0.6 copy.20
  243.6 0.0 copy-done
  243.6 0.6 reshape.38
  244.2 0.0 copy-start.1
  244.2 0.6 copy-done.1
  244.9 0.6 slice_bitcast_fusion
  245.5 1.6 copy.23
  (2 shorter events, 0.0 us)
Async XLA Ops:
  0.6 0.7 copy-start.2
  242.1 1.5 copy-start
  244.2 0.6 copy-start.1

commit v6 on v5

--- a/solution.py
+++ b/solution.py
@@ -126,11 +126,17 @@
         at = (owner * reps + rep) * piece + which * part_rows
         return wall.at[pl.ds(pl.multiple_of(at, 16), part_rows)]
 
-    def ring(src, wsrc, owner, step, way):
-        there = {"seq": right if way == 0 else left}
-        copy_to(src, slot(owner), ring_send.at[way, step], ring_recv.at[way, step], there).start()
+    def onward(way):
+        return {"seq": right if way == 0 else left}
+
+    def ring(src, owner, step, way):
         copy_to(
-            wsrc, wslot(owner, grp), wring_send.at[way, step], wring_recv.at[way, step], there
+            src, slot(owner), ring_send.at[way, step], ring_recv.at[way, step], onward(way)
+        ).start()
+
+    def wring(src, owner, step, way):
+        copy_to(
+            src, wslot(owner, grp), wring_send.at[way, step], wring_recv.at[way, step], onward(way)
         ).start()
 
     def aside(src, owner):
@@ -154,8 +160,9 @@
 
     own_rows = pl.ds(pl.multiple_of((me * reps + rep) * piece, 16), piece)
     own_part = w_ref.at[pl.ds(pl.multiple_of(grp * part_rows, 16), part_rows)]
-    ring(mine, own_part, me, 0, 0)
-    ring(mine, own_part, me, 0, 1)
+    for way in range(2):
+        ring(mine, me, 0, way)
+        wring(own_part, me, 0, way)
     aside(mine, me)
     to_sibling(w_ref, wall.at[own_rows])
     bcg[pl.ds(g * share, share), me] = bc_ref[pl.ds(g * share, share)]
@@ -172,13 +179,18 @@
     def send_x(to):
         copy_to(xs.at[to], xg.at[:, me], x_send, x_recv, {"seq": to}).start()
 
+    near = pairs // 5
+
     def pair_at(k):
         return lax.rem(my_pair + offset_of(k) + pairs, pairs)
+
+    def x_pair(k):
+        return pair_at(jnp.where(k < pairs - near, k + near, pairs - k))
 
     loads[2].wait()
     loads[3].wait()
     pack(my_pair)
-    pack(pair_at(1))
+    pack(x_pair(1))
     send_x(sibling)
     xg[:, me] = xs[me]
     dt_t = dt_ref[...].astype(f32).reshape(blocks * sub, n).T
@@ -187,28 +199,34 @@
     def lap(k, carry):
         @pl.when(k + 1 < pairs)
         def _():
-            pack(pair_at(k + 1))
+            pack(x_pair(k + 1))
 
         @pl.when(k < pairs)
         def _():
-            p = pair_at(k)
+            p = x_pair(k)
             send_x(2 * p)
             send_x(2 * p + 1)
 
         from_left, from_right = lax.rem(me - k + n, n), lax.rem(me + k, n)
         arrived(slot(from_left), ring_recv.at[0, k - 1], to_right)
-        arrived(wslot(from_left, grp), wring_recv.at[0, k - 1], to_right)
-        ring(slot(from_left), wslot(from_left, grp), from_left, k, 0)
-        aside(slot(from_left), from_left)
-        hand_on(from_left)
+        ring(slot(from_left), from_left, k, 0)
         arrived(slot(from_right), ring_recv.at[1, k - 1], to_right)
-        arrived(wslot(from_right, grp), wring_recv.at[1, k - 1], to_right)
 
         @pl.when(k < last_left)
         def _():
-            ring(slot(from_right), wslot(from_right, grp), from_right, k, 1)
-
+            ring(slot(from_right), from_right, k, 1)
+
+        arrived(wslot(from_left, grp), wring_recv.at[0, k - 1], to_right)
+        wring(wslot(from_left, grp), from_left, k, 0)
+        arrived(wslot(from_right, grp), wring_recv.at[1, k - 1], to_right)
+
+        @pl.when(k < last_left)
+        def _():
+            wring(wslot(from_right, grp), from_right, k, 1)
+
+        aside(slot(from_left), from_left)
         aside(slot(from_right), from_right)
+        hand_on(from_left)
         hand_on(from_right)
         return carry
 
@@ -482,7 +500,7 @@
             ms[:, h, :, part] = block.reshape(pairs, sub, LANES)
 
     def send_m(k, carry):
-        to = lax.rem(me + offset_of(k) + n, n)
+        to = lax.rem(me + offset_of(n - k) + n, n)
         copy_to(
             ms.at[lax.div(to, 2), lax.rem(to, 2)], mg.at[me], m_send, m_recv, {"seq": to}
         ).start()

time: 248 us -> 242 us (0.976)
  Pallas kernels: 238 us -> 231 us
    pallas_call x1, Pallas kernels: 238 us -> 231 us  [layer(): pl.pallas_call(layer_kernel, out_shape=(jax.ShapeDtypeStruct((span, cols)...]
where the time goes in v6:
time: 242 us; the launch traced here: 241 us
  Pallas kernels  231 us (95%)
  local copies, waits for them, and re-layouts  4.79 us (2%)
  between operations  3.27 us (1%)
    pallas_call x1, Pallas kernels, layer(): pl.pallas_call(layer_kernel, out_shape=(jax.ShapeDtypeStruct((span, cols)...  231 us

profile of v6, /device:TPU:40, one launch (start us, length us, event | category | flops | bytes accessed | tf_op | source)
XLA Modules:
  0.0 240.7 jit_solution(12594096614239457211)
XLA Ops:
  0.6 0.0 copy-start.2
  0.6 0.6 copy-done.2
  1.3 0.6 fusion
  4.5 231.2 %layer.1 = (bf16[128,512]{1,0:T(8,128)(2,1)}, f32[32,2,128]{2,1,0:T(2,128)}, bf16[4,128]{1,0:T(4,128)(2,1)}, bf16[4,256]{1,0:T(4,128)(2,1)}) custom-call(s32[1]{0:T(128)} %copy.22.start_ref, f32[32]{0:T(128)} %a_ref.1, f32[32]{0:T(128)} %bias_ref.1, f32[32]{0:T(128)} %skip_ref.1, s32[1,32]{1,0:T(1,128)} %owner_hbm.1, f32[4,2048]{1,0:T(4,128)} %taps_hbm.1, ...), custom_call_target="tpu_custom_call" | custom-call | flops 2000000000 | bytes 300000000 | tf_op jit(solution)/shard_map/layer/pallas_call | solution.py:563
  235.7 0.0 copy-start
  235.8 0.7 slice_select_fusion
  236.5 0.1 reshape.39
  236.6 0.6 copy.20
  237.2 0.0 copy-done
  237.2 0.6 reshape.38
  237.8 0.0 copy-start.1
  237.8 0.6 copy-done.1
  238.5 0.6 slice_bitcast_fusion
  239.1 1.6 copy.23
  (2 shorter events, 0.0 us)
Async XLA Ops:
  0.6 0.7 copy-start.2
  235.7 1.5 copy-start
  237.8 0.6 copy-start.1
